TPU v7x, 128 devices: a whole 4x4x4 slice. The times are simulated.
128 devices in a mesh: mesh: 32 (over y, x_lo, z), member: 4 (over x_hi, core).
Axes of the slice: x: 4 (x_hi: 2, x_lo: 2; x = x_hi * 2 + x_lo), y: 4, z: 4, core: 2. Of those that a mesh axis runs over, the one named last changes fastest.
Arguments:
- node_states: bfloat16 [8, 16384, 512], P('member', 'mesh'), may hold values from -60 to 60
- projection: bfloat16 [512, 1536], P('member'), may hold values from -12 to 12
- output_weight: bfloat16 [512, 512], P('member'), may hold values from -0.25 to 0.25
- up_weight: bfloat16 [512, 2048], P('member'), may hold values from -0.25 to 0.25
- down_weight: bfloat16 [2048, 512], P('member'), may hold values from -0.125 to 0.125
- attention_gain: float32 [512], replicated, may hold values from 0.5 to 2
- feedforward_gain: float32 [512], replicated, may hold values from 0.5 to 2
- tile_lists: int32 [128, 8], P('mesh'), may hold values from 0 to 127, as said below
- tile_counts: int32 [128], P('mesh'), may hold values from 4 to 8, as said below
Outputs:
- updated_states: bfloat16 [8, 16384, 512], P('member', 'mesh')
Inputs may be any that keep to these rules, and one draw needn't show every extreme that they name: `tile_lists`: entry 0 of tile t's list is t. Every entry names a tile of the device that holds t, or one of the last 4 tiles of the device before it, or one of the first 4 tiles of the device after it along mesh (the first and last devices are neighbours). The first tile_counts[t] entries are distinct; later entries are ignored. `tile_counts`: every device holds a tile whose count is 8.
All inputs are finite; a program needn't handle non-finite values.
Results may differ from a plain program's by a relative error of at most 0.0056.
Values may be sent and summed in bfloat16 or wider, within the bound.
A program may use at most 128 MiB of HBM per device.

v0:
```python
import math

import jax
import jax.numpy as jnp
from jax import lax
from jax.sharding import PartitionSpec as P

HEADS = 4
RIM_T = 4


def side_by_side(arrays, axis, dim, along):
    ends, at = ([], 0)
    for a in arrays[:-1]:
        at += a.shape[along]
        ends.append(at)
    both = jnp.concatenate(arrays, axis=along)
    return tuple(jnp.split(lax.all_gather(both, axis, axis=dim, tiled=True), ends, axis=along))


def extended(shard, sides, width):
    for axis, dim in sides:
        count, length = (lax.axis_size(axis), shard.shape[dim])
        up = [(i, (i + 1) % count) for i in range(count)]
        down = [(j, i) for i, j in up]
        last = lax.slice_in_dim(shard, length - width, length, axis=dim)
        leading = lax.slice_in_dim(shard, 0, width, axis=dim)
        before = lax.ppermute(last, axis, up)
        after = lax.ppermute(leading, axis, down)
        shard = jnp.concatenate([before, shard, after], axis=dim)
    return shard


def layer_norm(node_rows, gain):
    values = node_rows.astype(jnp.float32)
    center = values - jnp.mean(values, axis=-1, keepdims=True)
    spread = jnp.mean(center * center, axis=-1, keepdims=True)
    return (center * lax.rsqrt(spread + 1e-05) * gain).astype(jnp.bfloat16)


def attend(queries, window, tile_ids, counts):
    members, groups, tile_rows, model_width = queries.shape
    entries = tile_ids.shape[1]
    head_size = model_width // HEADS
    picked = jnp.take(window, tile_ids.reshape(-1), axis=1)
    picked = picked.reshape(members, groups, entries * tile_rows, 2 * model_width)
    key_part = picked[..., :model_width].reshape(
        members, groups, entries * tile_rows, HEADS, head_size
    )
    value_part = picked[..., model_width:].reshape(
        members, groups, entries * tile_rows, HEADS, head_size
    )
    query_part = queries.reshape(members, groups, tile_rows, HEADS, head_size)
    scores = jnp.einsum(
        "mgqhe,mgkhe->mghqk", query_part, key_part, preferred_element_type=jnp.float32
    ) / math.sqrt(head_size)
    usable = (jnp.arange(entries * tile_rows) // tile_rows)[None, :] < counts[:, None]
    scores = jnp.where(usable[None, :, None, None, :], scores, -jnp.inf)
    highest = jnp.max(scores, axis=-1, keepdims=True)
    weights = jnp.exp(scores - highest)
    summed = jnp.sum(weights, axis=-1, keepdims=True)
    rounded = weights.astype(jnp.bfloat16)
    blended = (
        jnp.einsum("mghqk,mgkhe->mghqe", rounded, value_part, preferred_element_type=jnp.float32)
        / summed
    )
    blended = jnp.transpose(blended, (0, 1, 3, 2, 4)).reshape(
        members, groups, tile_rows, model_width
    )
    return blended.astype(jnp.bfloat16)


def on_device(
    node_states,
    projection,
    output_weight,
    up_weight,
    down_weight,
    attention_gain,
    feedforward_gain,
    tile_lists,
    tile_counts,
):
    members, node_count, model_width = node_states.shape
    tiles_here = tile_lists.shape[0]
    tile_rows = node_count // tiles_here
    border_rows = RIM_T * tile_rows
    whole_projection, whole_output, whole_up, whole_down = (
        *side_by_side((projection, output_weight, up_weight), "member", 0, 1),
        lax.all_gather(down_weight, "member", axis=0, tiled=True),
    )
    normed = layer_norm(node_states, attention_gain)
    projected = jnp.dot(
        normed.reshape(-1, model_width), whole_projection, preferred_element_type=jnp.float32
    )
    projected = projected.reshape(members, node_count, 3 * model_width)
    queries = projected[..., :model_width].astype(jnp.bfloat16)
    pairs = projected[..., model_width:].astype(jnp.bfloat16)
    border = extended(normed, (("mesh", 1),), border_rows)
    pair_weight = whole_projection[:, model_width:]
    leading = jnp.einsum(
        "mnd,de->mne", border[:, :border_rows], pair_weight, preferred_element_type=jnp.float32
    ).astype(jnp.bfloat16)
    trailing = jnp.einsum(
        "mnd,de->mne",
        border[:, border_rows + node_count :],
        pair_weight,
        preferred_element_type=jnp.float32,
    ).astype(jnp.bfloat16)
    window = jnp.concatenate([leading, pairs, trailing], axis=1)
    window = window.reshape(members, tiles_here + 2 * RIM_T, tile_rows, 2 * model_width)
    all_tiles = tiles_here * lax.axis_size("mesh")
    first_tile = lax.axis_index("mesh") * tiles_here
    local_ids = jnp.mod(tile_lists - first_tile + RIM_T, all_tiles)
    grouped = jnp.transpose(
        queries.reshape(members, tiles_here // 2, 2, tile_rows, model_width), (1, 0, 2, 3, 4)
    )
    lists_grouped = local_ids.reshape(tiles_here // 2, 2, local_ids.shape[1])
    counts_grouped = tile_counts.reshape(tiles_here // 2, 2)

    def one_group(element):
        return attend(element[0], window, element[1], element[2])

    attended = lax.map(one_group, (grouped, lists_grouped, counts_grouped))
    attended = jnp.transpose(attended, (1, 0, 2, 3, 4)).reshape(-1, model_width)
    flat_states = node_states.reshape(-1, model_width)
    total_rows = flat_states.shape[0]
    block_rows = math.gcd(total_rows, 512)

    def finish(element):
        states, blended = element
        middle = (
            states.astype(jnp.float32)
            + jnp.dot(blended, whole_output, preferred_element_type=jnp.float32)
        ).astype(jnp.bfloat16)
        middle = lax.optimization_barrier(middle)
        normed_second = layer_norm(middle, feedforward_gain)
        hidden = jax.nn.gelu(
            jnp.dot(normed_second, whole_up, preferred_element_type=jnp.float32), approximate=True
        ).astype(jnp.bfloat16)
        return (
            middle.astype(jnp.float32)
            + jnp.dot(hidden, whole_down, preferred_element_type=jnp.float32)
        ).astype(jnp.bfloat16)

    result = lax.map(
        finish,
        (
            flat_states.reshape(-1, block_rows, model_width),
            attended.reshape(-1, block_rows, model_width),
        ),
    )
    return result


def solution(mesh):
    in_specs = (
        P("member", "mesh", None),
        P("member", None),
        P("member", None),
        P("member", None),
        P("member", None),
        P(),
        P(),
        P("mesh", None),
        P("mesh"),
    )
    out_specs = P("member", "mesh", None)
    return jax.shard_map(
        on_device, mesh=mesh, in_specs=in_specs, out_specs=out_specs, check_vma=False
    )
```

profile of v0, /device:TPU:1, one launch (start us, length us, event | category | flops | bytes accessed | tf_op | source)
XLA Modules:
  0.0 227.5 jit_solution(7013098283850008959)
XLA Ops:
  6.5 0.0 all-gather.3.cloned.1.call-start
  6.6 2.3 %pad_maximum_fusion.1 = bf16[128,4096]{1,0:T(8,128)(2,1)} fusion(bf16[128,2048]{1,0:T(8,128)(2,1)} %param.16, bf16[128,512]{1,0:T(8,128)(2,1)} %param.15, bf16[128,1536]{1,0:T(8,128)(2,1)} %param.14), kind=kLoop, calls=%fused_computation.85 | loop fusion | flops 3145728 | bytes 2097152 | tf_op jit(solution)/shard_map/concatenate | solution.py:17
  8.9 0.0 all-gather.3.cloned.1.call-update
  9.0 0.0 all-gather.5.cloned.1.call-start
  9.0 1.4 convert_reduce_fusion.1
  10.5 0.5 fusion.69
  11.0 0.4 fusion.71
  11.4 8.0 %collective-permute-start.1 = (bf16[2,512,512]{2,1,0:T(8,128)(2,1)S(1)}, bf16[2,512,512]{2,1,0:T(8,128)(2,1)}, u32[]{:S(2)}, u32[]{:S(2)}) collective-permute-start(bf16[2,512,512]{2,1,0:T(8,128)(2,1)S(1)} %fusion.71), channel_id=1, source_target_pairs={{4,0},{8,4},{12,8},{16,12},{20,16},{24,20},{28,24},{32,28},{36,32}... | collective-permute-start | bytes 3145736 | tf_op jit(solution)/shard_map/ppermute | solution.py:29
  19.4 0.0 collective-permute-start
  19.4 0.0 all-gather.5.cloned.1.call-update
  19.5 0.1 reshape.189
  19.6 50.2 %all-gather.3.cloned.1.call-done = bf16[512,4096]{1,0:T(8,128)(2,1)} async-done(((bf16[128,4096]{1,0:T(8,128)(2,1)}), bf16[512,4096]{1,0:T(8,128)(2,1)}) %all-gather.3.cloned.1.call-update) | async-done | bytes 4194320 | tf_op jit(solution)/shard_map/all_gather | solution.py:18
  69.8 3.2 %convolution_convert_fusion = bf16[2,512,1536]{2,1,0:T(8,128)(2,1)S(1)} fusion(bf16[2,512,512]{2,1,0:T(8,128)(2,1)S(1)} %fusion.71, bf16[512,4096]{1,0:T(8,128)(2,1)} %all-gather.3.cloned.1.call-done), kind=kOutput, calls=%fused_computation.73 | convolution fusion | flops 1612185600 | bytes 5767168 | tf_op jit(solution)/shard_map/dot_general | solution.py:93
  73.0 0.1 slice.31
  73.1 1.5 copy-done.4
  74.6 0.7 copy.23
  75.3 0.0 collective-permute-done.1
  75.3 2.9 %convolution_convert_fusion.1 = bf16[2,512,1024]{2,1,0:T(8,128)(2,1)S(1)} fusion(bf16[2,512,512]{2,1,0:T(8,128)(2,1)} %collective-permute-done.1, bf16[512,4096]{1,0:T(8,128)(2,1)} %all-gather.3.cloned.1.call-done), kind=kOutput, calls=%fused_computation.81 | convolution fusion | flops 1074790400 | bytes 4194304 | tf_op jit(solution)/shard_map/mnd,de->mne/dot_general | solution.py:104
  78.3 2.7 %convolution_convert_fusion.2 = bf16[2,512,1024]{2,1,0:T(8,128)(2,1)S(1)} fusion(bf16[2,512,512]{2,1,0:T(8,128)(2,1)} %collective-permute-done, bf16[512,4096]{1,0:T(8,128)(2,1)S(1)} %copy-done.3), kind=kOutput, calls=%fused_computation.82 | convolution fusion | flops 1074790400 | bytes 4194304 | tf_op jit(solution)/shard_map/mnd,de->mne/dot_general | solution.py:101
  81.0 9.3 %pad_maximum_fusion = bf16[2,1536,1024]{2,1,0:T(8,128)(2,1)} fusion(bf16[2,512,1024]{2,1,0:T(8,128)(2,1)S(1)} %convolution_convert_fusion.1, bf16[2,512,1024]{2,1,0:T(8,128)(2,1)S(1)} %slice-done.1, bf16[2,512,1024]{2,1,0:T(8,128)(2,1)S(1)} %convolution_convert_fusion.2), kind=kLoop, calls=%fused_computation.72 | loop fusion | flops 18874368 | bytes 12582912 | tf_op jit(solution)/shard_map/concatenate | solution.py:110
  90.3 111.5 %while.22 = (s32[]{:T(128)}, bf16[2,2,2,128,512]{3,4,2,1,0:T(8,128)(2,1)S(1)}, s32[2,2]{1,0:T(2,128)S(1)}, bf16[2,2,2,128,512]{3,4,2,1,0:T(8,128)(2,1)S(1)}, s32...) while((s32[]{:T(128)}, bf16[2,2,2,128,512]{3,4,2,1,0:T(8,128)(2,1)S(1)}, ...), condition=%wide.region_5.6_spmd, body=%wide.region_2.5_spmd.sunk | while | flops 1101536384 | bytes 154210992 | solution.py:124
  90.3 0.1 reshape.209
  90.4 7.5 %gather_fusion = bf16[16,2,128,1024]{3,2,1,0:T(8,128)(2,1)} fusion(bf16[2,12,128,1024]{3,2,1,0:T(8,128)(2,1)} %get-tuple-element.278, s32[1024]{0:T(1024)S(1)} %pad_clamp_fusion.2), kind=kCustom, calls=%fused_computation.clone.1 | custom fusion | bytes 16777280 | tf_op jit(solution)/shard_map/while/body/eval_jaxpr/jit(_take)/gather | solution.py:45
  97.9 8.2 %copy.35 = bf16[2,16,128,1024]{3,2,1,0:T(8,128)(2,1)} copy(bf16[2,16,128,1024]{3,2,0,1:T(8,128)(2,1)} %bitcast.101) | data formatting | bytes 16777216 | tf_op jit(solution)/shard_map/while/body/eval_jaxpr/jit(_take)/gather | solution.py:45
  106.1 0.1 broadcast_bitcast_fusion.2
  106.2 7.4 %bitcast_select_fusion.2 = bf16[2,2,1024,1024]{3,2,1,0:T(8,128)(2,1)} fusion(pred[2,1024]{1,0:T(4,128)(4,1)S(1)} %bitcast.111, bf16[2,2,1024,1024]{3,2,1,0:T(8,128)(2,1)} %bitcast.100), kind=kLoop, calls=%fused_computation.37.clone.1 | loop fusion | flops 4194304 | bytes 16779264 | tf_op jit(solution)/shard_map/while/body/eval_jaxpr/jit(_take)/select_n | solution.py:45
  113.6 5.7 %fusion.106 = (bf16[2,2,1024,512]{3,2,1,0:T(8,128)(2,1)}, bf16[2,2,1024,512]{3,2,1,0:T(8,128)(2,1)}) fusion(bf16[2,2,1024,1024]{3,2,1,0:T(8,128)(2,1)} %bitcast_select_fusion.2), kind=kLoop, calls=%fused_computation.92.clone.1 | loop fusion | bytes 16777216 | tf_op jit(solution)/shard_map/while/body/eval_jaxpr/slice | solution.py:47
  119.4 6.3 %copy.37 = bf16[2,2,1024,512]{2,3,1,0:T(8,128)(2,1)} copy(bf16[2,2,1024,512]{3,2,1,0:T(8,128)(2,1)} %get-tuple-element.248) | data formatting | bytes 8388608 | tf_op jit(solution)/shard_map/while/body/eval_jaxpr/slice | solution.py:47
  125.7 0.1 broadcast_compare_fusion.2
  125.8 3.7 %fusion.108 = (f32[2,2,4,128]{3,2,1,0:T(4,128)S(1)}, f32[2,2,4,128,1024]{4,3,2,1,0:T(8,128)S(1)}) fusion(pred[2,1024]{1,0:T(4,128)(4,1)S(1)} %broadcast_compare_fusion.2, bf16[2,2,128,4,128]{2,4,3,1,0:T(8,128)(2,1)S(1)} %bitcast.105, bf16[2,2,1024,4,128]{2,4,3,1,0:T(8,128)(2,1)} %bitcast.102), kind=kOutput, calls=%fused_computation.40.clone.1 | convolution fusion | flops 543160320 | bytes 13117440 | tf_op jit(solution)/shard_map/while/body/eval_jaxpr/mgqhe,mgkhe->mghqk/dot_general | solution.py:54
  129.5 2.0 fusion.109
  131.5 1.3 copy-done
  132.7 6.3 %copy.36 = bf16[2,2,1024,512]{2,3,1,0:T(8,128)(2,1)} copy(bf16[2,2,1024,512]{3,2,1,0:T(8,128)(2,1)} %get-tuple-element.247) | data formatting | bytes 8388608 | tf_op jit(solution)/shard_map/while/body/eval_jaxpr/slice | solution.py:50
  139.0 6.9 %divide_convert_fusion.2 = bf16[2,2,128,4,128]{2,4,3,1,0:T(8,128)(2,1)S(1)} fusion(bf16[2,2,1024,4,128]{2,4,3,1,0:T(8,128)(2,1)} %bitcast.104, f32[2,2,4,128,1024]{4,3,2,1,0:T(8,128)} %copy-done, f32[2,2,4,128]{3,2,1,0:T(4,128)S(1)} %get-tuple-element.250, pred[2,1024]{1,0:T(4,128)(4,1)S(1)} %broadcast_compare_fusion.2, ...), kind=kOutput, calls=%fused_computation.49.clone.1 | convolution fusion | flops 545783808 | bytes 13125632 | tf_op jit(solution)/shard_map/while/body/eval_jaxpr/mghqk,mgkhe->mghqe/dot_general | solution.py:64
  145.9 0.1 constant_dynamic-update-slice_fusion.2
  146.0 0.1 reshape.209
  146.1 7.5 %gather_fusion = bf16[16,2,128,1024]{3,2,1,0:T(8,128)(2,1)} fusion(bf16[2,12,128,1024]{3,2,1,0:T(8,128)(2,1)} %get-tuple-element.278, s32[1024]{0:T(1024)S(1)} %pad_clamp_fusion.2), kind=kCustom, calls=%fused_computation.clone.1 | custom fusion | bytes 16777280 | tf_op jit(solution)/shard_map/while/body/eval_jaxpr/jit(_take)/gather | solution.py:45
  153.7 8.2 %copy.35 = bf16[2,16,128,1024]{3,2,1,0:T(8,128)(2,1)} copy(bf16[2,16,128,1024]{3,2,0,1:T(8,128)(2,1)} %bitcast.101) | data formatting | bytes 16777216 | tf_op jit(solution)/shard_map/while/body/eval_jaxpr/jit(_take)/gather | solution.py:45
  161.9 0.1 broadcast_bitcast_fusion.2
  162.0 7.4 %bitcast_select_fusion.2 = bf16[2,2,1024,1024]{3,2,1,0:T(8,128)(2,1)} fusion(pred[2,1024]{1,0:T(4,128)(4,1)S(1)} %bitcast.111, bf16[2,2,1024,1024]{3,2,1,0:T(8,128)(2,1)} %bitcast.100), kind=kLoop, calls=%fused_computation.37.clone.1 | loop fusion | flops 4194304 | bytes 16779264 | tf_op jit(solution)/shard_map/while/body/eval_jaxpr/jit(_take)/select_n | solution.py:45
  169.4 5.7 %fusion.106 = (bf16[2,2,1024,512]{3,2,1,0:T(8,128)(2,1)}, bf16[2,2,1024,512]{3,2,1,0:T(8,128)(2,1)}) fusion(bf16[2,2,1024,1024]{3,2,1,0:T(8,128)(2,1)} %bitcast_select_fusion.2), kind=kLoop, calls=%fused_computation.92.clone.1 | loop fusion | bytes 16777216 | tf_op jit(solution)/shard_map/while/body/eval_jaxpr/slice | solution.py:47
  175.2 6.3 %copy.37 = bf16[2,2,1024,512]{2,3,1,0:T(8,128)(2,1)} copy(bf16[2,2,1024,512]{3,2,1,0:T(8,128)(2,1)} %get-tuple-element.248) | data formatting | bytes 8388608 | tf_op jit(solution)/shard_map/while/body/eval_jaxpr/slice | solution.py:47
  181.5 0.1 broadcast_compare_fusion.2
  181.6 3.7 %fusion.108 = (f32[2,2,4,128]{3,2,1,0:T(4,128)S(1)}, f32[2,2,4,128,1024]{4,3,2,1,0:T(8,128)S(1)}) fusion(pred[2,1024]{1,0:T(4,128)(4,1)S(1)} %broadcast_compare_fusion.2, bf16[2,2,128,4,128]{2,4,3,1,0:T(8,128)(2,1)S(1)} %bitcast.105, bf16[2,2,1024,4,128]{2,4,3,1,0:T(8,128)(2,1)} %bitcast.102), kind=kOutput, calls=%fused_computation.40.clone.1 | convolution fusion | flops 543160320 | bytes 13117440 | tf_op jit(solution)/shard_map/while/body/eval_jaxpr/mgqhe,mgkhe->mghqk/dot_general | solution.py:54
  185.3 2.0 fusion.109
  187.3 1.3 copy-done
  188.5 6.3 %copy.36 = bf16[2,2,1024,512]{2,3,1,0:T(8,128)(2,1)} copy(bf16[2,2,1024,512]{3,2,1,0:T(8,128)(2,1)} %get-tuple-element.247) | data formatting | bytes 8388608 | tf_op jit(solution)/shard_map/while/body/eval_jaxpr/slice | solution.py:50
  194.8 6.9 %divide_convert_fusion.2 = bf16[2,2,128,4,128]{2,4,3,1,0:T(8,128)(2,1)S(1)} fusion(bf16[2,2,1024,4,128]{2,4,3,1,0:T(8,128)(2,1)} %bitcast.104, f32[2,2,4,128,1024]{4,3,2,1,0:T(8,128)} %copy-done, f32[2,2,4,128]{3,2,1,0:T(4,128)S(1)} %get-tuple-element.250, pred[2,1024]{1,0:T(4,128)(4,1)S(1)} %broadcast_compare_fusion.2, ...), kind=kOutput, calls=%fused_computation.49.clone.1 | convolution fusion | flops 545783808 | bytes 13125632 | tf_op jit(solution)/shard_map/while/body/eval_jaxpr/mghqk,mgkhe->mghqe/dot_general | solution.py:64
  201.7 0.1 constant_dynamic-update-slice_fusion.2
  201.8 0.0 copy-start.2
  201.8 0.0 slice-start
  201.8 0.0 copy-start.9
  201.8 0.9 copy-done.6
  202.8 1.5 copy.24
  204.3 3.2 %split.14 = bf16[512,2048]{1,0:T(8,128)(2,1)} slice(bf16[512,4096]{1,0:T(8,128)(2,1)} %all-gather.3.cloned.1.call-done), slice={[0:512], [2048:4096]} | slice | bytes 4194304 | tf_op jit(solution)/shard_map/split | solution.py:18
  207.5 13.2 %while.23 = (s32[]{:T(128)}, bf16[2,512,512]{2,1,0:T(8,128)(2,1)}, bf16[2,512,512]{2,1,0:T(8,128)(2,1)S(1)}, bf16[2,512,512]{2,1,0:T(8,128)(2,1)S(1)}, bf16[512,...) while((s32[]{:T(128)}, bf16[2,512,512]{2,1,0:T(8,128)(2,1)}, ...), condition=%wide.region_9.10_spmd, body=%wide.region_6.9_spmd.sunk | while | flops 2429813248 | bytes 8935005 | solution.py:146
  207.5 0.4 fusion.116
  207.9 0.1 convert_reduce_fusion.3
  208.1 0.3 fusion.117
  208.4 5.7 %fusion.118 = bf16[2,512,512]{2,1,0:T(8,128)(2,1)} fusion(bf16[2,512,512]{2,1,0:T(8,128)(2,1)} %get-tuple-element.290, s32[]{:T(128)} %get-tuple-element.289, bf16[2048,512]{1,0:T(8,128)(2,1)} %get-tuple-element.305, bf16[512,512]{1,0:T(8,128)(2,1)S(1)} %fusion.116, bf16[512,2048]{1,0:T(8,128)(2,1)} %get-tuple-element.304, ...), kind=kOutput, calls=%fused_computation.20.clone.1 | convolution fusion | flops 2159017984 | bytes 5773824 | tf_op jit(solution)/shard_map/while/body/eval_jaxpr/dot_general | solution.py:143
  214.1 0.4 fusion.116
  214.5 0.1 convert_reduce_fusion.3
  214.7 0.3 fusion.117
  215.0 5.7 %fusion.118 = bf16[2,512,512]{2,1,0:T(8,128)(2,1)} fusion(bf16[2,512,512]{2,1,0:T(8,128)(2,1)} %get-tuple-element.290, s32[]{:T(128)} %get-tuple-element.289, bf16[2048,512]{1,0:T(8,128)(2,1)} %get-tuple-element.305, bf16[512,512]{1,0:T(8,128)(2,1)S(1)} %fusion.116, bf16[512,2048]{1,0:T(8,128)(2,1)} %get-tuple-element.304, ...), kind=kOutput, calls=%fused_computation.20.clone.1 | convolution fusion | flops 2159017984 | bytes 5773824 | tf_op jit(solution)/shard_map/while/body/eval_jaxpr/dot_general | solution.py:143
  (46 shorter events, 0.3 us)
Async XLA Ops:
  6.5 3.9 %copy-start.1 = (bf16[2,512,512]{2,1,0:T(8,128)(2,1)S(1)}, bf16[2,512,512]{2,1,0:T(8,128)(2,1)}, u32[]{:S(2)}) copy-start(bf16[2,512,512]{2,1,0:T(8,128)(2,1)} %param.13) | copy-start | bytes 3145732
  6.5 4.5 %copy-start.7 = (f32[512]{0:T(512)S(1)}, f32[512]{0:T(512)}, u32[]{:S(2)}) copy-start(f32[512]{0:T(512)} %param.18) | copy-start | bytes 6148
  6.5 13.0 %copy-start.10 = (s32[4]{0:T(128)S(1)}, s32[4]{0:T(128)}, u32[]{:S(2)}) copy-start(s32[4]{0:T(128)} %param.21) | copy-start | bytes 52
  6.5 13.0 %copy-start.8 = (s32[4,8]{1,0:T(4,128)S(1)}, s32[4,8]{1,0:T(4,128)}, u32[]{:S(2)}) copy-start(s32[4,8]{1,0:T(4,128)} %param.20) | copy-start | bytes 388
  6.5 63.3 %all-gather.3.cloned.1.call-start = ((), (), s32[]{:S(2)}) async-start(), calls=%async_computation | async-start | bytes 5242880 | tf_op jit(solution)/shard_map/all_gather | solution.py:18
  9.0 198.5 %all-gather.5.cloned.1.call-start = ((), (), s32[]{:S(2)}) async-start(), calls=%async_computation.1 | async-start | bytes 2621440 | tf_op jit(solution)/shard_map/all_gather | solution.py:90
  11.4 63.9 %collective-permute-start.1 = (bf16[2,512,512]{2,1,0:T(8,128)(2,1)S(1)}, bf16[2,512,512]{2,1,0:T(8,128)(2,1)}, u32[]{:S(2)}, u32[]{:S(2)}) collective-permute-start(bf16[2,512,512]{2,1,0:T(8,128)(2,1)S(1)} %fusion.71), channel_id=1, source_target_pairs={{4,0},{8,4},{12,8},{16,12},{20,16},{24,20},{28,24},{32,28},{36,32}... | collective-permute-start | bytes 3145736 | tf_op jit(solution)/shard_map/ppermute | solution.py:29
  19.4 58.8 %collective-permute-start = (bf16[2,512,512]{2,1,0:T(8,128)(2,1)S(1)}, bf16[2,512,512]{2,1,0:T(8,128)(2,1)}, u32[]{:S(2)}, u32[]{:S(2)}) collective-permute-start(bf16[2,512,512]{2,1,0:T(8,128)(2,1)S(1)} %fusion.71), channel_id=1, source_target_pairs={{0,4},{4,8},{8,12},{12,16},{16,20},{20,24},{24,28},{28,32},{32,36}... | collective-permute-start | bytes 3145736 | tf_op jit(solution)/shard_map/ppermute | solution.py:28
  73.0 1.6 copy-start.4
  75.3 3.0 %copy-start.3 = (bf16[512,4096]{1,0:T(8,128)(2,1)S(1)}, bf16[512,4096]{1,0:T(8,128)(2,1)}, u32[]{:S(2)}) copy-start(bf16[512,4096]{1,0:T(8,128)(2,1)} %all-gather.3.cloned.1.call-done) | copy-start | bytes 12582916
  78.3 2.7 %slice-start.1 = ((bf16[2,512,1536]{2,1,0:T(8,128)(2,1)}), bf16[2,512,1024]{2,1,0:T(8,128)(2,1)S(1)}, s32[]{:S(2)}) async-start(bf16[2,512,1536]{2,1,0:T(8,128)(2,1)} %copy-done.4), calls=%async_computation.3 | async-start | bytes 4194304 | tf_op jit(solution)/shard_map/slice | solution.py:98
  81.0 9.3 %copy-start.5 = (bf16[2,2,2,128,512]{3,4,2,1,0:T(8,128)(2,1)S(1)}, bf16[2,2,2,128,512]{3,4,2,1,0:T(8,128)(2,1)}, u32[]{:S(2)}) copy-start(bf16[2,2,2,128,512]{3,4,2,1,0:T(8,128)(2,1)} %custom-call.2) | copy-start | bytes 3145732
  129.5 3.2 %copy-start = (f32[2,2,4,128,1024]{4,3,2,1,0:T(8,128)}, f32[2,2,4,128,1024]{4,3,2,1,0:T(8,128)S(1)}, u32[]{:S(2)}) copy-start(f32[2,2,4,128,1024]{4,3,2,1,0:T(8,128)S(1)} %get-tuple-element.249) | copy-start | bytes 25165828 | tf_op jit(solution)/shard_map/while
  185.3 3.2 %copy-start = (f32[2,2,4,128,1024]{4,3,2,1,0:T(8,128)}, f32[2,2,4,128,1024]{4,3,2,1,0:T(8,128)S(1)}, u32[]{:S(2)}) copy-start(f32[2,2,4,128,1024]{4,3,2,1,0:T(8,128)S(1)} %get-tuple-element.249) | copy-start | bytes 25165828 | tf_op jit(solution)/shard_map/while
  201.8 1.0 copy-start.6
  201.8 5.6 %copy-start.2 = (bf16[2,512,512]{2,1,0:T(8,128)(2,1)S(1)}, bf16[2,512,512]{2,1,0:T(8,128)(2,1)}, u32[]{:S(2)}) copy-start(bf16[2,512,512]{2,1,0:T(8,128)(2,1)} %param.13) | copy-start | bytes 3145732
  201.8 5.6 %slice-start = ((bf16[512,4096]{1,0:T(8,128)(2,1)}), bf16[512,512]{1,0:T(8,128)(2,1)S(1)}, s32[]{:S(2)}) async-start(bf16[512,4096]{1,0:T(8,128)(2,1)} %all-gather.3.cloned.1.call-done), calls=%async_computation.2 | async-start | bytes 1048576 | tf_op jit(solution)/shard_map/split | solution.py:18
  201.8 5.6 %copy-start.9 = (f32[512]{0:T(512)S(1)}, f32[512]{0:T(512)}, u32[]{:S(2)}) copy-start(f32[512]{0:T(512)} %param.19) | copy-start | bytes 6148
Sparse Core Ops, SparseCore 0:
  9.1 60.6 all-gather.2
  71.5 25.7 all-gather.4
where the time goes:
time: 229 us; the launch traced here: 228 us
  local copies, waits for them, and re-layouts  79.1 us (35%)
  waiting for transfers between devices  50.2 us (22%)
  matrix products  42.4 us (19%)
  other arithmetic  33.9 us (15%)
  between operations  13.6 us (6%)
  starting transfers between devices  8.1 us (4%)
    all_gather x1, waiting for transfers between devices, side_by_side(): lax.all_gather(both, axis, axis=dim, tiled=True)  50.2 us
    gather x4, local copies, waits for them, and re-layouts, attend(): picked = jnp.take(window, tile_ids.reshape(-1), axis=1)  31.5 us
    slice x4, local copies, waits for them, and re-layouts, attend(): picked[..., :model_width]  24 us
    select_n x4, other arithmetic, attend(): picked = jnp.take(window, tile_ids.reshape(-1), axis=1)  14.9 us
    dot_general x2, matrix products, attend(): jnp.einsum('mghqk,mgkhe->mghqe', rounded, value_part, preferred_element_t...  13.8 us
    slice x2, local copies, waits for them, and re-layouts, attend(): picked[..., model_width:]  12.5 us
    dot_general x2, matrix products, finish(): jnp.dot(hidden, whole_down, preferred_element_type=jnp.float32)  11.4 us
    concatenate x1, other arithmetic, on_device(): window = jnp.concatenate([leading, pairs, trailing], axis=1)  9.26 us
  transfers between devices with their start and end apart: 4, of which 1 were waited for; matrix products, arithmetic and copies ran while one was open for 59% of the time, Pallas kernels for 0%

commit v1 on v0

v1 whole, which is shorter than its diff:
```python
import functools
import math

import jax
import jax.numpy as jnp
from jax import lax
from jax.experimental import pallas as pl
from jax.experimental.pallas import tpu as pltpu
from jax.sharding import PartitionSpec as P

HEADS = 4
TILE = 128
RIM_T = 4
HIDDEN_LOW = -1e30
MESH = pl.DeviceIdType.MESH
F32 = jnp.float32
BF16 = jnp.bfloat16

SPLIT = ((0, 2), (1, 1), (2, 2), (3, 2))


def normed(values, gain):
    values = values.astype(F32)
    center = values - jnp.mean(values, axis=-1, keepdims=True)
    spread = jnp.mean(center * center, axis=-1, keepdims=True)
    return (center * lax.rsqrt(spread + 1e-05) * gain).astype(BF16)


def dot_nn(a, b):
    return jnp.dot(a, b, preferred_element_type=F32)


def dot_nt(a, b):
    return lax.dot_general(a, b, (((1,), (1,)), ((), ())), preferred_element_type=F32)


def dot_tn(a, b):
    return lax.dot_general(a, b, (((0,), (0,)), ((), ())), preferred_element_type=F32)


def layer_kernel(
    geometry,
    x_hbm, wp_hbm, wo_hbm, wu_hbm, wd_hbm, gain1, gain2, lists, counts,
    out_ref,
    own, halo, wp, wo, wu, wd, wq_t, wv_t, xn, hn, q_t, kc, v_t, acc, top, total, bias, scores, hid,
    loc_sem, halo_send, halo_recv, p_send, p_recv,
    x_send, x_recv, y_send, y_recv, dx_send, dx_recv, dy_send, dy_recv,
):
    n_mesh, n_z, n_x, n_member = geometry
    members, rows, width = x_hbm.shape
    tiles = rows // TILE
    head = width // HEADS
    i = lax.axis_index("mesh")
    m = lax.axis_index("member")
    nxt = (i + 1) % n_mesh
    prv = (i + n_mesh - 1) % n_mesh
    x_lo = (i // n_z) % n_x
    y = i // (n_z * n_x)
    half = y % 2
    plane = n_z * n_x
    cross = (i + n_z - 2 * n_z * x_lo, (m + 2) % n_member)
    mate = (i, m + 1 - 2 * (m % 2))
    y_to = ((i + n_mesh + plane * (2 * x_lo - 1)) % n_mesh, m)
    y_from = ((i + n_mesh - plane * (2 * x_lo - 1)) % n_mesh, m)
    far = (m + 2) % n_member
    mate_far = (mate[1] + 2) % n_member

    barrier = pltpu.get_barrier_semaphore()
    for peer in ((nxt, m), (prv, m), cross, mate, y_to, y_from):
        pl.semaphore_signal(barrier, inc=1, device_id=peer, device_id_type=MESH)

    sources = (wp_hbm, wo_hbm, wu_hbm, wd_hbm)
    fulls = (wp, wo, wu, wd)

    def shard(w, owner):
        r = sources[w].shape[0]
        return fulls[w].at[pl.ds(pl.multiple_of(owner * r, 16), r), :]

    def piece(w, n, k, owner, which):
        r = sources[w].shape[0]
        size = r // 2 // n
        start = owner * r + which * (r // 2) + k * size
        return fulls[w].at[pl.ds(pl.multiple_of(start, 16), size), :]

    load_x = pltpu.make_async_copy(x_hbm, own, loc_sem.at[4])
    load_x.start()
    loads = [pltpu.make_async_copy(sources[w], shard(w, m), loc_sem.at[w]) for w in range(4)]
    for load in loads:
        load.start()

    pieces = []
    for w, n in SPLIT:
        for k in range(n):
            pieces.append((w, n, k))

    def remote(src, dst, send, recv, peer):
        return pltpu.make_async_remote_copy(
            src_ref=src, dst_ref=dst, send_sem=send, recv_sem=recv, device_id=peer, device_id_type=MESH
        )

    def halo_copy(side, b, j):
        src = own.at[b, pl.ds(pl.multiple_of(j * TILE, TILE), TILE), :]
        dst = halo.at[b, side, pl.ds(pl.multiple_of(j * TILE, TILE), TILE), :]
        peer = (nxt, m) if side == 0 else (prv, m)
        return remote(src, dst, halo_send.at[side, b, j], halo_recv.at[side, b, j], peer)

    def mate_copy(w, owner):
        return remote(shard(w, owner), shard(w, owner), p_send.at[w], p_recv.at[w], mate)

    def x_copy(p, owner):
        ref = piece(*pieces[p], owner, half)
        return remote(ref, ref, x_send.at[p], x_recv.at[p], cross)

    def y_copy(p, which):
        ref = piece(*pieces[p], far, which)
        return remote(ref, ref, y_send.at[p], y_recv.at[p], y_to)

    def dx_copy(p, owner):
        ref = piece(*pieces[p], owner, half)
        return remote(ref, ref, dx_send.at[p], dx_recv.at[p], mate)

    def dy_copy(p, owner):
        ref = piece(*pieces[p], owner, 1 - half)
        return remote(ref, ref, dy_send.at[p], dy_recv.at[p], mate)

    def pass_x(p):
        x_copy(p, far).wait_recv()
        y_copy(p, half).start()
        dx_copy(p, far).start()

    def pass_y(p):
        y_copy(p, 1 - half).wait_recv()
        dy_copy(p, far).start()

    def arrive(w):
        mate_copy(w, mate[1]).wait_recv()
        for p, entry in enumerate(pieces):
            if entry[0] == w:
                dx_copy(p, mate_far).wait_recv()
                dy_copy(p, mate_far).wait_recv()

    first = i * tiles - RIM_T
    all_tiles = n_mesh * tiles
    entries = lists.shape[1]
    locals_ = [[(lists[t, e] - first + all_tiles) % all_tiles for e in range(entries)] for t in range(tiles)]
    for kt in range(tiles + 2 * RIM_T):
        for t in range(tiles):
            hit = jnp.int32(0)
            for e in range(entries):
                used = jnp.logical_and(locals_[t][e] == kt, e < counts[t])
                hit = jnp.where(used, jnp.int32(1), hit)
            level = jnp.where(hit > 0, F32(0), F32(HIDDEN_LOW))
            bias[pl.ds(kt, 1), t * TILE:(t + 1) * TILE] = jnp.full((1, TILE), level, F32)

    load_x.wait()
    for load in loads:
        load.wait()
    pl.semaphore_wait(barrier, 6)

    for b in range(members):
        for j in range(tiles):
            for side in range(2):
                halo_copy(side, b, j).start()
    for w in range(4):
        for p, entry in enumerate(pieces):
            if entry[0] == w:
                x_copy(p, m).start()
        mate_copy(w, m).start()

    def norm_own(k, _):
        b = k // tiles
        at = pl.ds(pl.multiple_of((k % tiles) * TILE, TILE), TILE)
        xn[b, at, :] = normed(own[b, at, :], gain1[...])
        return 0

    lax.fori_loop(0, members * tiles, norm_own, 0)

    pass_x(0)
    pass_x(1)
    pass_x(2)
    pass_y(0)
    pass_y(1)
    arrive(0)
    wq_t[...] = jnp.transpose(wp[:, :width])
    wv_t[...] = jnp.transpose(wp[:, 2 * width:])
    scale = F32(math.log2(math.e) / math.sqrt(head))

    def project(source, n):
        keys = dot_nn(source[...], wp[:, width:2 * width]).astype(BF16)
        for h in range(HEADS):
            kc[h, :n, :] = keys[:, h * head:(h + 1) * head]
        v_t[:, :n] = dot_nt(wv_t[...], source[...]).astype(BF16)

    def attend(marks, opening):
        n = len(marks) * TILE
        for h in range(HEADS):
            feats = slice(h * head, (h + 1) * head)
            scores[h, :n, :] = dot_nn(kc[h, :n, :], q_t[feats, :])
        for h in range(HEADS):
            feats = slice(h * head, (h + 1) * head)
            best = None if opening else top[h]
            for k, mark in enumerate(marks):
                high = jnp.max(scores[h, k * TILE:(k + 1) * TILE, :], axis=0, keepdims=True) + mark
                best = high if best is None else jnp.maximum(best, high)
            parts, added = [], None
            for k, mark in enumerate(marks):
                part = jnp.exp2(scores[h, k * TILE:(k + 1) * TILE, :] - (best - mark))
                summed = jnp.sum(part, axis=0, keepdims=True)
                added = summed if added is None else added + summed
                parts.append(part.astype(BF16))
            product = dot_nn(v_t[feats, :n], jnp.concatenate(parts, axis=0))
            if opening:
                acc[h] = product
                total[h] = added
            else:
                fade = jnp.exp2(top[h] - best)
                acc[h] = acc[h] * fade + product
                total[h] = total[h] * fade + added
            top[h] = best

    def one_member(b, _):
        q_t[...] = (dot_nt(wq_t[...], xn[b]) * scale).astype(BF16)
        project(xn.at[b], rows)
        attend([bias[RIM_T + t:RIM_T + t + 1, :] for t in range(tiles)], True)

        @pl.when(b == 0)
        def _():
            pass_x(3)
            pass_x(4)
            pass_y(2)

        def one_step(j, _):
            for side in range(2):
                halo_copy(side, b, j).wait_recv()
                at = pl.ds(pl.multiple_of(j * TILE, TILE), TILE)
                hn[side * TILE:(side + 1) * TILE, :] = normed(halo[b, side, at, :], gain1[...])
            project(hn, 2 * TILE)
            attend([bias[pl.ds(j, 1), :], bias[pl.ds(j + RIM_T + tiles, 1), :]], False)

            @pl.when(jnp.logical_and(b == 0, j == 0))
            def _():
                pass_y(3)
                pass_x(5)

            @pl.when(jnp.logical_and(b == 0, j == 1))
            def _():
                pass_y(4)

            @pl.when(jnp.logical_and(b == 0, j == 2))
            def _():
                pass_x(6)
                pass_y(5)

            @pl.when(jnp.logical_and(b == 0, j == 3))
            def _():
                pass_y(6)
                arrive(1)
                arrive(2)
                arrive(3)

            return 0

        lax.fori_loop(0, tiles, one_step, 0)

        for h in range(HEADS):
            v_t[h * head:(h + 1) * head, :] = (acc[h] / total[h]).astype(BF16)

        def finish(r, _):
            block = rows // 2
            at = pl.ds(pl.multiple_of(r * block, block), block)
            middle = (own[b, at, :].astype(F32) + dot_tn(v_t[:, at], wo[...])).astype(BF16)
            second = normed(middle, gain2[...])
            inner = wu.shape[1]
            step = inner // 4
            for f in range(4):
                u = dot_nn(second, wu[:, f * step:(f + 1) * step])
                slope = math.sqrt(2.0 / math.pi)
                bent = jnp.tanh(u * (slope + (slope * 0.044715) * (u * u)))
                hid[:, f * step:(f + 1) * step] = (0.5 * u * (1.0 + bent)).astype(BF16)
            out_ref[b, at, :] = (middle.astype(F32) + dot_nn(hid[...], wd[...])).astype(BF16)
            return 0

        lax.fori_loop(0, 2, finish, 0)
        return 0

    lax.fori_loop(0, members, one_member, 0)

    for b in range(members):
        for j in range(tiles):
            for side in range(2):
                halo_copy(side, b, j).wait_send()
    for w in range(4):
        mate_copy(w, m).wait_send()
    for p in range(len(pieces)):
        x_copy(p, m).wait_send()
        y_copy(p, half).wait_send()
        dx_copy(p, far).wait_send()
        dy_copy(p, far).wait_send()


def solution(mesh):
    n_mesh, n_member = mesh.shape["mesh"], mesh.shape["member"]
    geometry = (n_mesh, 4, 2, n_member)

    def on_device(states, projection, output_w, up_w, down_w, gain1, gain2, lists, counts):
        members, rows, width = states.shape
        inner = up_w.shape[1]
        tiles = rows // TILE
        n_pieces = sum(n for _, n in SPLIT)
        hbm = pl.BlockSpec(memory_space=pl.ANY)
        vmem = pl.BlockSpec(memory_space=pltpu.VMEM)
        smem = pl.BlockSpec(memory_space=pltpu.SMEM)
        dma = pltpu.SemaphoreType.DMA
        return pl.pallas_call(
            functools.partial(layer_kernel, geometry),
            name="layer",
            out_shape=jax.ShapeDtypeStruct(states.shape, BF16),
            in_specs=[hbm] * 5 + [vmem] * 2 + [smem] * 2,
            out_specs=vmem,
            scratch_shapes=[
                pltpu.VMEM((members, rows, width), BF16),
                pltpu.VMEM((members, 2, rows, width), BF16),
                pltpu.VMEM((width, 3 * width), BF16),
                pltpu.VMEM((width, width), BF16),
                pltpu.VMEM((width, inner), BF16),
                pltpu.VMEM((inner, width), BF16),
                pltpu.VMEM((width, width), BF16),
                pltpu.VMEM((width, width), BF16),
                pltpu.VMEM((members, rows, width), BF16),
                pltpu.VMEM((2 * TILE, width), BF16),
                pltpu.VMEM((width, rows), BF16),
                pltpu.VMEM((HEADS, rows, width // HEADS), BF16),
                pltpu.VMEM((width, rows), BF16),
                pltpu.VMEM((HEADS, width // HEADS, rows), F32),
                pltpu.VMEM((HEADS, 1, rows), F32),
                pltpu.VMEM((HEADS, 1, rows), F32),
                pltpu.VMEM((tiles + 2 * RIM_T, rows), F32),
                pltpu.VMEM((HEADS, rows, rows), F32),
                pltpu.VMEM((rows // 2, inner), BF16),
                dma((5,)),
                dma((2, members, tiles)), dma((2, members, tiles)),
                dma((4,)), dma((4,)),
            ] + [dma((n_pieces,)) for _ in range(8)],
            compiler_params=pltpu.CompilerParams(
                collective_id=0, has_side_effects=True, vmem_limit_bytes=60 * 1024 * 1024
            ),
        )(
            states, projection, output_w, up_w, down_w,
            gain1.reshape(1, width), gain2.reshape(1, width), lists, counts,
        )

    in_specs = (
        P("member", "mesh", None),
        P("member", None),
        P("member", None),
        P("member", None),
        P("member", None),
        P(),
        P(),
        P("mesh", None),
        P("mesh"),
    )
    return jax.shard_map(
        on_device, mesh=mesh, in_specs=in_specs, out_specs=P("member", "mesh", None), check_vma=False
    )
```

time: 229 us -> 58 us (0.25)
  local copies, waits for them, and re-layouts: 79.1 us -> 2.26 us
  Pallas kernels: 0 us -> 55.5 us
  waiting for transfers between devices: 50.2 us -> 0 us
  matrix products: 42.4 us -> 0 us
  other arithmetic: 33.9 us -> 0 us
  between operations: 13.6 us -> 0.01 us
  starting transfers between devices: 8.1 us -> 0 us
    pallas_call x0 -> x1, Pallas kernels: none -> 55.5 us  [on_device(): pl.pallas_call(functools.partial(layer_kernel, geometry), name='layer', o...]
    all_gather x2 -> x0, waiting for transfers between devices: 50.2 us -> none  [the longest x1 50.2 us: side_by_side(): lax.all_gather(both, axis, axis=dim, tiled=True)]
    dot_general x11 -> x0, matrix products: 42.4 us -> none  [the longest x2 13.8 us: attend(): jnp.einsum('mghqk,mgkhe->mghqe', rounded, value_part, preferred_element_t...]
    slice x9 -> x0, local copies, waits for them, and re-layouts: 36.6 us -> none  [the longest x4 24 us: attend(): picked[..., :model_width]]
    gather x4 -> x0, local copies, waits for them, and re-layouts: 31.5 us -> none  [attend(): picked = jnp.take(window, tile_ids.reshape(-1), axis=1)]
    select_n x7 -> x0, other arithmetic: 14.9 us -> none  [the longest x4 14.9 us: attend(): picked = jnp.take(window, tile_ids.reshape(-1), axis=1)]
    concatenate x2 -> x0, other arithmetic: 11.6 us -> none  [the longest x1 9.26 us: on_device(): window = jnp.concatenate([leading, pairs, trailing], axis=1)]
    ppermute x2 -> x0, starting transfers between devices: 8.02 us -> none  [the longest x1 8.02 us: extended(): after = lax.ppermute(leading, axis, down)]
  transfers between devices with their start and end apart: 4 -> 0, of which waited for: 1 -> 0; matrix products, arithmetic and copies ran while one was open for 59% -> 0% of each run, Pallas kernels for 0% -> 0%
where the time goes in v1:
time: 58 us; the launch traced here: 57.8 us
  Pallas kernels  55.5 us (96%)
  local copies, waits for them, and re-layouts  2.26 us (4%)
    pallas_call x1, Pallas kernels, on_device(): pl.pallas_call(functools.partial(layer_kernel, geometry), name='layer', o...  55.5 us
    unnamed x1, local copies, waits for them, and re-layouts  2.26 us

profile of v1, /device:TPU:1, one launch (start us, length us, event | category | flops | bytes accessed | tf_op | source)
XLA Modules:
  0.0 57.8 jit_solution(11160321678100654865)
XLA Ops:
  0.0 55.5 %layer.1 = bf16[2,512,512]{2,1,0:T(8,128)(2,1)} custom-call(bf16[2,512,512]{2,1,0:T(8,128)(2,1)} %x_hbm.1, bf16[128,1536]{1,0:T(8,128)(2,1)} %wp_hbm.1, bf16[128,512]{1,0:T(8,128)(2,1)} %wo_hbm.1, bf16[128,2048]{1,0:T(8,128)(2,1)} %wu_hbm.1, bf16[512,512]{1,0:T(8,128)(2,1)} %wd_hbm.1, f32[1,512]{1,0:T(1,128)} %bitcast.2, f32[1,512]{1,0:T(1,128)} %bitcast.3, ...), custom_call_target="tpu_custom_call" | custom-call | tf_op jit(solution)/shard_map/layer/pallas_call | solution.py:314
  55.5 2.3 %copy.11 = bf16[2,512,512]{2,1,0:T(8,128)(2,1)} copy(bf16[2,512,512]{2,1,0:T(8,128)(2,1)} %layer.1) | data formatting | bytes 2097152

commit v2 on v1

--- a/solution.py
+++ b/solution.py
@@ -40,9 +40,10 @@
 
 def layer_kernel(
     geometry,
-    x_hbm, wp_hbm, wo_hbm, wu_hbm, wd_hbm, gain1, gain2, lists, counts,
+    x_hbm, wp_hbm, wo_hbm, wu_hbm, wd_hbm, gain1_hbm, gain2_hbm, lists_hbm, counts_hbm,
     out_ref,
     own, halo, wp, wo, wu, wd, wq_t, wv_t, xn, hn, q_t, kc, v_t, acc, top, total, bias, scores, hid,
+    gain1, gain2, lists, counts,
     loc_sem, halo_send, halo_recv, p_send, p_recv,
     x_send, x_recv, y_send, y_recv, dx_send, dx_recv, dy_send, dy_recv,
 ):
@@ -82,6 +83,14 @@
         start = owner * r + which * (r // 2) + k * size
         return fulls[w].at[pl.ds(pl.multiple_of(start, 16), size), :]
 
+    smalls = [
+        pltpu.make_async_copy(src, dst, loc_sem.at[5 + k])
+        for k, (src, dst) in enumerate(
+            ((lists_hbm, lists), (counts_hbm, counts), (gain1_hbm, gain1), (gain2_hbm, gain2))
+        )
+    ]
+    for small in smalls:
+        small.start()
     load_x = pltpu.make_async_copy(x_hbm, own, loc_sem.at[4])
     load_x.start()
     loads = [pltpu.make_async_copy(sources[w], shard(w, m), loc_sem.at[w]) for w in range(4)]
@@ -139,6 +148,8 @@
                 dx_copy(p, mate_far).wait_recv()
                 dy_copy(p, mate_far).wait_recv()
 
+    for small in smalls:
+        small.wait()
     first = i * tiles - RIM_T
     all_tiles = n_mesh * tiles
     entries = lists.shape[1]
@@ -152,10 +163,11 @@
             level = jnp.where(hit > 0, F32(0), F32(HIDDEN_LOW))
             bias[pl.ds(kt, 1), t * TILE:(t + 1) * TILE] = jnp.full((1, TILE), level, F32)
 
-    load_x.wait()
-    for load in loads:
-        load.wait()
-    pl.semaphore_wait(barrier, 6)
+    with jax.named_scope("enter"):
+        load_x.wait()
+        for load in loads:
+            load.wait()
+        pl.semaphore_wait(barrier, 6)
 
     for b in range(members):
         for j in range(tiles):
@@ -173,32 +185,50 @@
         xn[b, at, :] = normed(own[b, at, :], gain1[...])
         return 0
 
-    lax.fori_loop(0, members * tiles, norm_own, 0)
-
-    pass_x(0)
-    pass_x(1)
-    pass_x(2)
-    pass_y(0)
-    pass_y(1)
-    arrive(0)
-    wq_t[...] = jnp.transpose(wp[:, :width])
-    wv_t[...] = jnp.transpose(wp[:, 2 * width:])
+    with jax.named_scope("norm_own"):
+        lax.fori_loop(0, members * tiles, norm_own, 0)
+
+    steps = members * tiles
+
+    def halo_norm(s, slot):
+        b, j = s // tiles, s % tiles
+        at = pl.ds(pl.multiple_of(j * TILE, TILE), TILE)
+        for side in range(2):
+            hn[slot, side * TILE:(side + 1) * TILE, :] = normed(halo[b, side, at, :], gain1[...])
+
+    def halo_wait(s):
+        for side in range(2):
+            halo_copy(side, s // tiles, s % tiles).wait_recv()
+
+    with jax.named_scope("gather"):
+        pass_x(0)
+        pass_x(1)
+        halo_wait(0)
+        halo_norm(0, 0)
+        pass_x(2)
+        pass_y(0)
+        pass_y(1)
+        pass_x(3)
+        arrive(0)
+    with jax.named_scope("flip"):
+        wq_t[...] = jnp.transpose(wp[:, :width])
+        wv_t[...] = jnp.transpose(wp[:, 2 * width:])
     scale = F32(math.log2(math.e) / math.sqrt(head))
 
-    def project(source, n):
+    def project(source, slot, n):
         keys = dot_nn(source[...], wp[:, width:2 * width]).astype(BF16)
         for h in range(HEADS):
-            kc[h, :n, :] = keys[:, h * head:(h + 1) * head]
-        v_t[:, :n] = dot_nt(wv_t[...], source[...]).astype(BF16)
-
-    def attend(marks, opening):
+            kc[slot, h, :n, :] = keys[:, h * head:(h + 1) * head]
+        v_t[slot, :, :n] = dot_nt(wv_t[...], source[...]).astype(BF16)
+
+    def attend(b, slot, marks, opening):
         n = len(marks) * TILE
         for h in range(HEADS):
             feats = slice(h * head, (h + 1) * head)
-            scores[h, :n, :] = dot_nn(kc[h, :n, :], q_t[feats, :])
+            scores[h, :n, :] = dot_nn(kc[slot, h, :n, :], q_t[b, feats, :])
         for h in range(HEADS):
             feats = slice(h * head, (h + 1) * head)
-            best = None if opening else top[h]
+            best = None if opening else top[b, h]
             for k, mark in enumerate(marks):
                 high = jnp.max(scores[h, k * TILE:(k + 1) * TILE, :], axis=0, keepdims=True) + mark
                 best = high if best is None else jnp.maximum(best, high)
@@ -208,82 +238,111 @@
                 summed = jnp.sum(part, axis=0, keepdims=True)
                 added = summed if added is None else added + summed
                 parts.append(part.astype(BF16))
-            product = dot_nn(v_t[feats, :n], jnp.concatenate(parts, axis=0))
+            product = dot_nn(v_t[slot, feats, :n], jnp.concatenate(parts, axis=0))
             if opening:
-                acc[h] = product
-                total[h] = added
+                acc[b, h] = product
+                total[b, h] = added
             else:
-                fade = jnp.exp2(top[h] - best)
-                acc[h] = acc[h] * fade + product
-                total[h] = total[h] * fade + added
-            top[h] = best
-
-    def one_member(b, _):
-        q_t[...] = (dot_nt(wq_t[...], xn[b]) * scale).astype(BF16)
-        project(xn.at[b], rows)
-        attend([bias[RIM_T + t:RIM_T + t + 1, :] for t in range(tiles)], True)
-
-        @pl.when(b == 0)
-        def _():
-            pass_x(3)
-            pass_x(4)
-            pass_y(2)
-
-        def one_step(j, _):
-            for side in range(2):
-                halo_copy(side, b, j).wait_recv()
-                at = pl.ds(pl.multiple_of(j * TILE, TILE), TILE)
-                hn[side * TILE:(side + 1) * TILE, :] = normed(halo[b, side, at, :], gain1[...])
-            project(hn, 2 * TILE)
-            attend([bias[pl.ds(j, 1), :], bias[pl.ds(j + RIM_T + tiles, 1), :]], False)
-
-            @pl.when(jnp.logical_and(b == 0, j == 0))
+                fade = jnp.exp2(top[b, h] - best)
+                acc[b, h] = acc[b, h] * fade + product
+                total[b, h] = total[b, h] * fade + added
+            top[b, h] = best
+
+    def own_project(b):
+        q_t[b] = (dot_nt(wq_t[...], xn[b]) * scale).astype(BF16)
+        project(xn.at[b], b, rows)
+
+    def own_attend(b):
+        attend(b, b, [bias[RIM_T + t:RIM_T + t + 1, :] for t in range(tiles)], True)
+
+    def halo_project(slot):
+        project(hn.at[slot], slot, 2 * TILE)
+
+    def halo_attend(s, slot):
+        b, j = s // tiles, s % tiles
+        attend(b, slot, [bias[pl.ds(j, 1), :], bias[pl.ds(j + RIM_T + tiles, 1), :]], False)
+
+    with jax.named_scope("own0"):
+        own_project(0)
+    with jax.named_scope("own1"):
+        own_attend(0)
+        own_project(1)
+    pass_x(4)
+    pass_y(2)
+    with jax.named_scope("wait1"):
+        halo_wait(1)
+    with jax.named_scope("own2"):
+        own_attend(1)
+        halo_project(0)
+        halo_norm(1, 1)
+
+    def two_steps(t, _):
+        s = 2 * t
+        with jax.named_scope("wait2"):
+            halo_wait(s + 2)
+
+            @pl.when(t == 0)
             def _():
                 pass_y(3)
                 pass_x(5)
 
-            @pl.when(jnp.logical_and(b == 0, j == 1))
+            @pl.when(t == 1)
             def _():
                 pass_y(4)
-
-            @pl.when(jnp.logical_and(b == 0, j == 2))
+                pass_y(5)
+
+        with jax.named_scope("stepa"):
+            halo_attend(s, 0)
+            halo_project(1)
+            halo_norm(s + 2, 0)
+        with jax.named_scope("wait3"):
+            halo_wait(s + 3)
+
+            @pl.when(t == 0)
             def _():
                 pass_x(6)
-                pass_y(5)
-
-            @pl.when(jnp.logical_and(b == 0, j == 3))
+
+            @pl.when(t == 2)
             def _():
                 pass_y(6)
-                arrive(1)
-                arrive(2)
-                arrive(3)
-
-            return 0
-
-        lax.fori_loop(0, tiles, one_step, 0)
-
-        for h in range(HEADS):
-            v_t[h * head:(h + 1) * head, :] = (acc[h] / total[h]).astype(BF16)
-
-        def finish(r, _):
-            block = rows // 2
-            at = pl.ds(pl.multiple_of(r * block, block), block)
-            middle = (own[b, at, :].astype(F32) + dot_tn(v_t[:, at], wo[...])).astype(BF16)
-            second = normed(middle, gain2[...])
-            inner = wu.shape[1]
-            step = inner // 4
-            for f in range(4):
-                u = dot_nn(second, wu[:, f * step:(f + 1) * step])
-                slope = math.sqrt(2.0 / math.pi)
-                bent = jnp.tanh(u * (slope + (slope * 0.044715) * (u * u)))
-                hid[:, f * step:(f + 1) * step] = (0.5 * u * (1.0 + bent)).astype(BF16)
-            out_ref[b, at, :] = (middle.astype(F32) + dot_nn(hid[...], wd[...])).astype(BF16)
-            return 0
-
-        lax.fori_loop(0, 2, finish, 0)
+
+        with jax.named_scope("stepb"):
+            halo_attend(s + 1, 1)
+            halo_project(0)
+            halo_norm(s + 3, 1)
         return 0
 
-    lax.fori_loop(0, members, one_member, 0)
+    lax.fori_loop(0, steps // 2 - 1, two_steps, 0)
+    with jax.named_scope("last"):
+        halo_attend(steps - 2, 0)
+        halo_project(1)
+        halo_attend(steps - 1, 1)
+    with jax.named_scope("gather2"):
+        arrive(1)
+        arrive(2)
+        arrive(3)
+
+    block = rows // 2
+    inner = wu.shape[1]
+    step = inner // 4
+    slope = math.sqrt(2.0 / math.pi)
+
+    def finish(b, _):
+        with jax.named_scope("finish"):
+            for h in range(HEADS):
+                v_t[0, h * head:(h + 1) * head, :] = (acc[b, h] / total[b, h]).astype(BF16)
+            for r in range(2):
+                at = slice(r * block, (r + 1) * block)
+                middle = (own[b, at, :].astype(F32) + dot_tn(v_t[0, :, at], wo[...])).astype(BF16)
+                second = normed(middle, gain2[...])
+                for f in range(4):
+                    u = dot_nn(second, wu[:, f * step:(f + 1) * step])
+                    bent = jnp.tanh(u * (slope + (slope * 0.044715) * (u * u)))
+                    hid[r, :, f * step:(f + 1) * step] = (0.5 * u * (1.0 + bent)).astype(BF16)
+                out_ref[b, at, :] = (middle.astype(F32) + dot_nn(hid[r], wd[...])).astype(BF16)
+        return 0
+
+    lax.fori_loop(0, members, finish, 0)
 
     for b in range(members):
         for j in range(tiles):
@@ -309,13 +368,12 @@
         n_pieces = sum(n for _, n in SPLIT)
         hbm = pl.BlockSpec(memory_space=pl.ANY)
         vmem = pl.BlockSpec(memory_space=pltpu.VMEM)
-        smem = pl.BlockSpec(memory_space=pltpu.SMEM)
         dma = pltpu.SemaphoreType.DMA
         return pl.pallas_call(
             functools.partial(layer_kernel, geometry),
             name="layer",
             out_shape=jax.ShapeDtypeStruct(states.shape, BF16),
-            in_specs=[hbm] * 5 + [vmem] * 2 + [smem] * 2,
+            in_specs=[hbm] * 9,
             out_specs=vmem,
             scratch_shapes=[
                 pltpu.VMEM((members, rows, width), BF16),
@@ -327,17 +385,19 @@
                 pltpu.VMEM((width, width), BF16),
                 pltpu.VMEM((width, width), BF16),
                 pltpu.VMEM((members, rows, width), BF16),
-                pltpu.VMEM((2 * TILE, width), BF16),
-                pltpu.VMEM((width, rows), BF16),
-                pltpu.VMEM((HEADS, rows, width // HEADS), BF16),
-                pltpu.VMEM((width, rows), BF16),
-                pltpu.VMEM((HEADS, width // HEADS, rows), F32),
-                pltpu.VMEM((HEADS, 1, rows), F32),
-                pltpu.VMEM((HEADS, 1, rows), F32),
+                pltpu.VMEM((2, 2 * TILE, width), BF16),
+                pltpu.VMEM((members, width, rows), BF16),
+                pltpu.VMEM((2, HEADS, rows, width // HEADS), BF16),
+                pltpu.VMEM((2, width, rows), BF16),
+                pltpu.VMEM((members, HEADS, width // HEADS, rows), F32),
+                pltpu.VMEM((members, HEADS, 1, rows), F32),
+                pltpu.VMEM((members, HEADS, 1, rows), F32),
                 pltpu.VMEM((tiles + 2 * RIM_T, rows), F32),
                 pltpu.VMEM((HEADS, rows, rows), F32),
-                pltpu.VMEM((rows // 2, inner), BF16),
-                dma((5,)),
+                pltpu.VMEM((2, rows // 2, inner), BF16),
+                pltpu.VMEM((1, width), F32), pltpu.VMEM((1, width), F32),
+                pltpu.SMEM(lists.shape, jnp.int32), pltpu.SMEM(counts.shape, jnp.int32),
+                dma((9,)),
                 dma((2, members, tiles)), dma((2, members, tiles)),
                 dma((4,)), dma((4,)),
             ] + [dma((n_pieces,)) for _ in range(8)],

time: 58 us -> 48.4 us (0.83)
  Pallas kernels: 55.5 us -> 46 us
    pallas_call x1, Pallas kernels: 55.5 us -> 46 us  [on_device(): pl.pallas_call(functools.partial(layer_kernel, geometry), name='layer', o...]
where the time goes in v2:
time: 48.4 us; the launch traced here: 48.3 us
  Pallas kernels  46 us (95%)
  local copies, waits for them, and re-layouts  2.26 us (5%)
    pallas_call x1, Pallas kernels, on_device(): pl.pallas_call(functools.partial(layer_kernel, geometry), name='layer', o...  46 us
    unnamed x1, local copies, waits for them, and re-layouts  2.26 us

profile of v2, /device:TPU:1, one launch (start us, length us, event | category | flops | bytes accessed | tf_op | source)
XLA Modules:
  0.0 48.3 jit_solution(8446016705233733719)
XLA Ops:
  0.0 46.0 %layer.1 = bf16[2,512,512]{2,1,0:T(8,128)(2,1)} custom-call(bf16[2,512,512]{2,1,0:T(8,128)(2,1)} %x_hbm.1, bf16[128,1536]{1,0:T(8,128)(2,1)} %wp_hbm.1, bf16[128,512]{1,0:T(8,128)(2,1)} %wo_hbm.1, bf16[128,2048]{1,0:T(8,128)(2,1)} %wu_hbm.1, bf16[512,512]{1,0:T(8,128)(2,1)} %wd_hbm.1, f32[1,512]{1,0:T(1,128)} %bitcast.2, f32[1,512]{1,0:T(1,128)} %bitcast.3, ...), custom_call_target="tpu_custom_call" | custom-call | tf_op jit(solution)/shard_map/layer/pallas_call | solution.py:372
  46.0 2.3 %copy.11 = bf16[2,512,512]{2,1,0:T(8,128)(2,1)} copy(bf16[2,512,512]{2,1,0:T(8,128)(2,1)} %layer.1) | data formatting | bytes 2097152

commit v3 on v2

--- a/solution.py
+++ b/solution.py
@@ -12,11 +12,13 @@
 TILE = 128
 RIM_T = 4
 HIDDEN_LOW = -1e30
+ONES = 16
+WEIGHT_TYPE = jnp.float32
 MESH = pl.DeviceIdType.MESH
 F32 = jnp.float32
 BF16 = jnp.bfloat16
 
-SPLIT = ((0, 2), (1, 1), (2, 2), (3, 2))
+SPLIT = ((0, 4), (1, 1), (2, 2), (3, 2))
 
 
 def normed(values, gain):
@@ -42,7 +44,7 @@
     geometry,
     x_hbm, wp_hbm, wo_hbm, wu_hbm, wd_hbm, gain1_hbm, gain2_hbm, lists_hbm, counts_hbm,
     out_ref,
-    own, halo, wp, wo, wu, wd, wq_t, wv_t, xn, hn, q_t, kc, v_t, acc, top, total, bias, scores, hid,
+    own, halo, wp, wo, wu, wd, wq_t, wv_t, xn, hn, q_t, kc, v_t, acc, top, bias, scores, hid, blend,
     gain1, gain2, lists, counts,
     loc_sem, halo_send, halo_recv, p_send, p_recv,
     x_send, x_recv, y_send, y_recv, dx_send, dx_recv, dy_send, dy_recv,
@@ -83,18 +85,17 @@
         start = owner * r + which * (r // 2) + k * size
         return fulls[w].at[pl.ds(pl.multiple_of(start, 16), size), :]
 
+    loads = [pltpu.make_async_copy(sources[w], shard(w, m), loc_sem.at[w]) for w in range(4)]
+    load_x = pltpu.make_async_copy(x_hbm, own, loc_sem.at[4])
     smalls = [
         pltpu.make_async_copy(src, dst, loc_sem.at[5 + k])
         for k, (src, dst) in enumerate(
             ((lists_hbm, lists), (counts_hbm, counts), (gain1_hbm, gain1), (gain2_hbm, gain2))
         )
     ]
-    for small in smalls:
-        small.start()
-    load_x = pltpu.make_async_copy(x_hbm, own, loc_sem.at[4])
+    loads[0].start()
     load_x.start()
-    loads = [pltpu.make_async_copy(sources[w], shard(w, m), loc_sem.at[w]) for w in range(4)]
-    for load in loads:
+    for load in loads[1:] + smalls:
         load.start()
 
     pieces = []
@@ -148,6 +149,24 @@
                 dx_copy(p, mate_far).wait_recv()
                 dy_copy(p, mate_far).wait_recv()
 
+    with jax.named_scope("enter"):
+        pl.semaphore_wait(barrier, 6)
+        loads[0].wait()
+    for p, entry in enumerate(pieces):
+        if entry[0] == 0:
+            x_copy(p, m).start()
+    mate_copy(0, m).start()
+    load_x.wait()
+    for b in range(members):
+        for j in range(tiles):
+            for side in range(2):
+                halo_copy(side, b, j).start()
+    for w in range(1, 4):
+        loads[w].wait()
+        for p, entry in enumerate(pieces):
+            if entry[0] == w:
+                x_copy(p, m).start()
+        mate_copy(w, m).start()
     for small in smalls:
         small.wait()
     first = i * tiles - RIM_T
@@ -163,22 +182,6 @@
             level = jnp.where(hit > 0, F32(0), F32(HIDDEN_LOW))
             bias[pl.ds(kt, 1), t * TILE:(t + 1) * TILE] = jnp.full((1, TILE), level, F32)
 
-    with jax.named_scope("enter"):
-        load_x.wait()
-        for load in loads:
-            load.wait()
-        pl.semaphore_wait(barrier, 6)
-
-    for b in range(members):
-        for j in range(tiles):
-            for side in range(2):
-                halo_copy(side, b, j).start()
-    for w in range(4):
-        for p, entry in enumerate(pieces):
-            if entry[0] == w:
-                x_copy(p, m).start()
-        mate_copy(w, m).start()
-
     def norm_own(k, _):
         b = k // tiles
         at = pl.ds(pl.multiple_of((k % tiles) * TILE, TILE), TILE)
@@ -203,23 +206,36 @@
     with jax.named_scope("gather"):
         pass_x(0)
         pass_x(1)
+        pass_x(2)
+        pass_y(0)
+        pass_x(3)
+        pass_y(1)
+        pass_y(2)
+        pass_x(4)
+        pass_y(3)
         halo_wait(0)
         halo_norm(0, 0)
-        pass_x(2)
-        pass_y(0)
-        pass_y(1)
-        pass_x(3)
+        pass_x(5)
         arrive(0)
     with jax.named_scope("flip"):
         wq_t[...] = jnp.transpose(wp[:, :width])
         wv_t[...] = jnp.transpose(wp[:, 2 * width:])
     scale = F32(math.log2(math.e) / math.sqrt(head))
 
+    for slot in range(2):
+        for h in range(HEADS):
+            v_t[slot, h, head:, :] = jnp.ones((ONES, rows), BF16)
+
+    def weights_of(lowered):
+        return jnp.exp2(lowered.astype(WEIGHT_TYPE)).astype(BF16)
+
     def project(source, slot, n):
         keys = dot_nn(source[...], wp[:, width:2 * width]).astype(BF16)
         for h in range(HEADS):
             kc[slot, h, :n, :] = keys[:, h * head:(h + 1) * head]
-        v_t[slot, :, :n] = dot_nt(wv_t[...], source[...]).astype(BF16)
+        values = dot_nt(wv_t[...], source[...]).astype(BF16)
+        for h in range(HEADS):
+            v_t[slot, h, :head, :n] = values[h * head:(h + 1) * head, :]
 
     def attend(b, slot, marks, opening):
         n = len(marks) * TILE
@@ -232,20 +248,14 @@
             for k, mark in enumerate(marks):
                 high = jnp.max(scores[h, k * TILE:(k + 1) * TILE, :], axis=0, keepdims=True) + mark
                 best = high if best is None else jnp.maximum(best, high)
-            parts, added = [], None
-            for k, mark in enumerate(marks):
-                part = jnp.exp2(scores[h, k * TILE:(k + 1) * TILE, :] - (best - mark))
-                summed = jnp.sum(part, axis=0, keepdims=True)
-                added = summed if added is None else added + summed
-                parts.append(part.astype(BF16))
-            product = dot_nn(v_t[slot, feats, :n], jnp.concatenate(parts, axis=0))
+            parts = [
+                weights_of(scores[h, k * TILE:(k + 1) * TILE, :] - (best - mark)) for k, mark in enumerate(marks)
+            ]
+            product = dot_nn(v_t[slot, h, :, :n], jnp.concatenate(parts, axis=0))
             if opening:
                 acc[b, h] = product
-                total[b, h] = added
             else:
-                fade = jnp.exp2(top[b, h] - best)
-                acc[b, h] = acc[b, h] * fade + product
-                total[b, h] = total[b, h] * fade + added
+                acc[b, h] = acc[b, h] * jnp.exp2(top[b, h] - best) + product
             top[b, h] = best
 
     def own_project(b):
@@ -267,8 +277,8 @@
     with jax.named_scope("own1"):
         own_attend(0)
         own_project(1)
-    pass_x(4)
-    pass_y(2)
+    pass_x(6)
+    pass_y(4)
     with jax.named_scope("wait1"):
         halo_wait(1)
     with jax.named_scope("own2"):
@@ -283,13 +293,16 @@
 
             @pl.when(t == 0)
             def _():
-                pass_y(3)
-                pass_x(5)
+                pass_y(5)
+                pass_x(7)
 
             @pl.when(t == 1)
             def _():
-                pass_y(4)
-                pass_y(5)
+                pass_y(6)
+
+            @pl.when(t == 2)
+            def _():
+                pass_y(7)
 
         with jax.named_scope("stepa"):
             halo_attend(s, 0)
@@ -300,11 +313,11 @@
 
             @pl.when(t == 0)
             def _():
-                pass_x(6)
+                pass_x(8)
 
             @pl.when(t == 2)
             def _():
-                pass_y(6)
+                pass_y(8)
 
         with jax.named_scope("stepb"):
             halo_attend(s + 1, 1)
@@ -327,22 +340,30 @@
     step = inner // 4
     slope = math.sqrt(2.0 / math.pi)
 
-    def finish(b, _):
-        with jax.named_scope("finish"):
+    def residual(b, r):
+        at = slice(r * block, (r + 1) * block)
+        return (own[b, at, :].astype(F32) + dot_tn(blend[b, :, at], wo[...])).astype(BF16)
+
+    def feed(b, r, middle):
+        at = slice(r * block, (r + 1) * block)
+        second = normed(middle, gain2[...])
+        for f in range(4):
+            u = dot_nn(second, wu[:, f * step:(f + 1) * step])
+            bent = jnp.tanh(u * (slope + (slope * 0.044715) * (u * u)))
+            hid[r, :, f * step:(f + 1) * step] = (u + u * bent).astype(BF16)
+        out_ref[b, at, :] = (middle.astype(F32) + 0.5 * dot_nn(hid[r], wd[...])).astype(BF16)
+
+    with jax.named_scope("finish"):
+        for b in range(members):
             for h in range(HEADS):
-                v_t[0, h * head:(h + 1) * head, :] = (acc[b, h] / total[b, h]).astype(BF16)
-            for r in range(2):
-                at = slice(r * block, (r + 1) * block)
-                middle = (own[b, at, :].astype(F32) + dot_tn(v_t[0, :, at], wo[...])).astype(BF16)
-                second = normed(middle, gain2[...])
-                for f in range(4):
-                    u = dot_nn(second, wu[:, f * step:(f + 1) * step])
-                    bent = jnp.tanh(u * (slope + (slope * 0.044715) * (u * u)))
-                    hid[r, :, f * step:(f + 1) * step] = (0.5 * u * (1.0 + bent)).astype(BF16)
-                out_ref[b, at, :] = (middle.astype(F32) + dot_nn(hid[r], wd[...])).astype(BF16)
-        return 0
-
-    lax.fori_loop(0, members, finish, 0)
+                inverse = 1.0 / acc[b, h, head:head + 1, :]
+                blend[b, h * head:(h + 1) * head, :] = (acc[b, h, :head, :] * inverse).astype(BF16)
+        jobs = [(b, r) for b in range(members) for r in range(2)]
+        middle = residual(*jobs[0])
+        for k, job in enumerate(jobs):
+            later = residual(*jobs[k + 1]) if k + 1 < len(jobs) else None
+            feed(*job, middle)
+            middle = later
 
     for b in range(members):
         for j in range(tiles):
@@ -372,7 +393,7 @@
         return pl.pallas_call(
             functools.partial(layer_kernel, geometry),
             name="layer",
-            out_shape=jax.ShapeDtypeStruct(states.shape, BF16),
+            out_shape=pltpu.VMEM(states.shape, BF16),
             in_specs=[hbm] * 9,
             out_specs=vmem,
             scratch_shapes=[
@@ -388,13 +409,13 @@
                 pltpu.VMEM((2, 2 * TILE, width), BF16),
                 pltpu.VMEM((members, width, rows), BF16),
                 pltpu.VMEM((2, HEADS, rows, width // HEADS), BF16),
-                pltpu.VMEM((2, width, rows), BF16),
-                pltpu.VMEM((members, HEADS, width // HEADS, rows), F32),
-                pltpu.VMEM((members, HEADS, 1, rows), F32),
+                pltpu.VMEM((2, HEADS, width // HEADS + ONES, rows), BF16),
+                pltpu.VMEM((members, HEADS, width // HEADS + ONES, rows), F32),
                 pltpu.VMEM((members, HEADS, 1, rows), F32),
                 pltpu.VMEM((tiles + 2 * RIM_T, rows), F32),
                 pltpu.VMEM((HEADS, rows, rows), F32),
                 pltpu.VMEM((2, rows // 2, inner), BF16),
+                pltpu.VMEM((members, width, rows), BF16),
                 pltpu.VMEM((1, width), F32), pltpu.VMEM((1, width), F32),
                 pltpu.SMEM(lists.shape, jnp.int32), pltpu.SMEM(counts.shape, jnp.int32),
                 dma((9,)),

time: 48.4 us -> 44.1 us (0.911)
  Pallas kernels: 46 us -> 43 us
  local copies, waits for them, and re-layouts: 2.26 us -> 0.97 us
    pallas_call x1, Pallas kernels: 46 us -> 43 us  [on_device(): pl.pallas_call(functools.partial(layer_kernel, geometry), name='layer', o...]
    unnamed x1, local copies, waits for them, and re-layouts: 2.26 us -> 0.97 us
where the time goes in v3:
time: 44.1 us; the launch traced here: 44 us
  Pallas kernels  43 us (98%)
  local copies, waits for them, and re-layouts  0.97 us (2%)
    pallas_call x1, Pallas kernels, on_device(): pl.pallas_call(functools.partial(layer_kernel, geometry), name='layer', o...  43 us
    unnamed x1, local copies, waits for them, and re-layouts  0.97 us

profile of v3, /device:TPU:1, one launch (start us, length us, event | category | flops | bytes accessed | tf_op | source)
XLA Modules:
  0.0 44.0 jit_solution(15945558873204818468)
XLA Ops:
  0.0 43.0 %layer.1 = bf16[2,512,512]{2,1,0:T(8,128)(2,1)S(1)} custom-call(bf16[2,512,512]{2,1,0:T(8,128)(2,1)} %x_hbm.1, bf16[128,1536]{1,0:T(8,128)(2,1)} %wp_hbm.1, bf16[128,512]{1,0:T(8,128)(2,1)} %wo_hbm.1, bf16[128,2048]{1,0:T(8,128)(2,1)} %wu_hbm.1, bf16[512,512]{1,0:T(8,128)(2,1)} %wd_hbm.1, f32[1,512]{1,0:T(1,128)} %bitcast.2, f32[1,512]{1,0:T(1,128)} %bitcast.3, ...), custom_call_target="tpu_custom_call" | custom-call | tf_op jit(solution)/shard_map/layer/pallas_call | solution.py:393
  43.0 1.0 %copy.11 = bf16[2,512,512]{2,1,0:T(8,128)(2,1)} copy(bf16[2,512,512]{2,1,0:T(8,128)(2,1)S(1)} %layer.1) | data formatting | bytes 2097152

commit v4 on v3

--- a/solution.py
+++ b/solution.py
@@ -18,7 +18,8 @@
 F32 = jnp.float32
 BF16 = jnp.bfloat16
 
-SPLIT = ((0, 4), (1, 1), (2, 2), (3, 2))
+SPLIT = ((0, 2), (1, 2), (2, 2), (3, 1), (4, 2), (5, 4))
+KEYS, VALUES, QUERIES, OUTPUT, UP, DOWN = range(6)
 
 
 def normed(values, gain):
@@ -44,7 +45,8 @@
     geometry,
     x_hbm, wp_hbm, wo_hbm, wu_hbm, wd_hbm, gain1_hbm, gain2_hbm, lists_hbm, counts_hbm,
     out_ref,
-    own, halo, wp, wo, wu, wd, wq_t, wv_t, xn, hn, q_t, kc, v_t, acc, top, bias, scores, hid, blend,
+    own, halo, wk, wv, wq, wo, wu, wd, wq_t, wv_t, xn, hn, q_t, kc, v_t, acc, top, bias, scores, hid, blend,
+    second, mid,
     gain1, gain2, lists, counts,
     loc_sem, halo_send, halo_recv, p_send, p_recv,
     x_send, x_recv, y_send, y_recv, dx_send, dx_recv, dy_send, dy_recv,
@@ -72,8 +74,12 @@
     for peer in ((nxt, m), (prv, m), cross, mate, y_to, y_from):
         pl.semaphore_signal(barrier, inc=1, device_id=peer, device_id_type=MESH)
 
-    sources = (wp_hbm, wo_hbm, wu_hbm, wd_hbm)
-    fulls = (wp, wo, wu, wd)
+    sources = (
+        wp_hbm.at[:, pl.ds(width, width)], wp_hbm.at[:, pl.ds(2 * width, width)], wp_hbm.at[:, pl.ds(0, width)],
+        wo_hbm, wu_hbm, wd_hbm,
+    )
+    fulls = (wk, wv, wq, wo, wu, wd)
+    n_weights = len(fulls)
 
     def shard(w, owner):
         r = sources[w].shape[0]
@@ -85,17 +91,15 @@
         start = owner * r + which * (r // 2) + k * size
         return fulls[w].at[pl.ds(pl.multiple_of(start, 16), size), :]
 
-    loads = [pltpu.make_async_copy(sources[w], shard(w, m), loc_sem.at[w]) for w in range(4)]
-    load_x = pltpu.make_async_copy(x_hbm, own, loc_sem.at[4])
+    loads = [pltpu.make_async_copy(sources[w], shard(w, m), loc_sem.at[w]) for w in range(n_weights)]
+    load_x = pltpu.make_async_copy(x_hbm, own, loc_sem.at[n_weights])
     smalls = [
-        pltpu.make_async_copy(src, dst, loc_sem.at[5 + k])
+        pltpu.make_async_copy(src, dst, loc_sem.at[n_weights + 1 + k])
         for k, (src, dst) in enumerate(
             ((lists_hbm, lists), (counts_hbm, counts), (gain1_hbm, gain1), (gain2_hbm, gain2))
         )
     ]
-    loads[0].start()
-    load_x.start()
-    for load in loads[1:] + smalls:
+    for load in loads[:3] + [load_x] + loads[3:] + smalls:
         load.start()
 
     pieces = []
@@ -149,24 +153,26 @@
                 dx_copy(p, mate_far).wait_recv()
                 dy_copy(p, mate_far).wait_recv()
 
+    def send_weight(w):
+        loads[w].wait()
+        for p, entry in enumerate(pieces):
+            if entry[0] == w:
+                x_copy(p, m).start()
+        mate_copy(w, m).start()
+
     with jax.named_scope("enter"):
         pl.semaphore_wait(barrier, 6)
-        loads[0].wait()
-    for p, entry in enumerate(pieces):
-        if entry[0] == 0:
-            x_copy(p, m).start()
-    mate_copy(0, m).start()
+    send_weight(KEYS)
+    send_weight(VALUES)
+    send_weight(QUERIES)
     load_x.wait()
     for b in range(members):
         for j in range(tiles):
             for side in range(2):
                 halo_copy(side, b, j).start()
-    for w in range(1, 4):
-        loads[w].wait()
-        for p, entry in enumerate(pieces):
-            if entry[0] == w:
-                x_copy(p, m).start()
-        mate_copy(w, m).start()
+    send_weight(OUTPUT)
+    send_weight(UP)
+    send_weight(DOWN)
     for small in smalls:
         small.wait()
     first = i * tiles - RIM_T
@@ -203,39 +209,27 @@
         for side in range(2):
             halo_copy(side, s // tiles, s % tiles).wait_recv()
 
-    with jax.named_scope("gather"):
-        pass_x(0)
-        pass_x(1)
-        pass_x(2)
-        pass_y(0)
-        pass_x(3)
-        pass_y(1)
-        pass_y(2)
-        pass_x(4)
-        pass_y(3)
-        halo_wait(0)
-        halo_norm(0, 0)
-        pass_x(5)
-        arrive(0)
-    with jax.named_scope("flip"):
-        wq_t[...] = jnp.transpose(wp[:, :width])
-        wv_t[...] = jnp.transpose(wp[:, 2 * width:])
     scale = F32(math.log2(math.e) / math.sqrt(head))
 
-    for slot in range(2):
+    for slot in range(3):
         for h in range(HEADS):
             v_t[slot, h, head:, :] = jnp.ones((ONES, rows), BF16)
 
     def weights_of(lowered):
         return jnp.exp2(lowered.astype(WEIGHT_TYPE)).astype(BF16)
 
-    def project(source, slot, n):
-        keys = dot_nn(source[...], wp[:, width:2 * width]).astype(BF16)
+    def project_keys(source, slot, n):
+        keys = dot_nn(source[...], wk[...]).astype(BF16)
         for h in range(HEADS):
             kc[slot, h, :n, :] = keys[:, h * head:(h + 1) * head]
+
+    def project_values(source, slot, n):
         values = dot_nt(wv_t[...], source[...]).astype(BF16)
         for h in range(HEADS):
             v_t[slot, h, :head, :n] = values[h * head:(h + 1) * head, :]
+
+    def project_queries(b):
+        q_t[b] = (dot_nt(wq_t[...], xn[b]) * scale).astype(BF16)
 
     def attend(b, slot, marks, opening):
         n = len(marks) * TILE
@@ -258,118 +252,172 @@
                 acc[b, h] = acc[b, h] * jnp.exp2(top[b, h] - best) + product
             top[b, h] = best
 
-    def own_project(b):
-        q_t[b] = (dot_nt(wq_t[...], xn[b]) * scale).astype(BF16)
-        project(xn.at[b], b, rows)
-
     def own_attend(b):
-        attend(b, b, [bias[RIM_T + t:RIM_T + t + 1, :] for t in range(tiles)], True)
-
-    def halo_project(slot):
-        project(hn.at[slot], slot, 2 * TILE)
-
-    def halo_attend(s, slot):
+        attend(b, 1 + b, [bias[RIM_T + t:RIM_T + t + 1, :] for t in range(tiles)], True)
+
+    def halo_project(s):
+        project_keys(hn.at[s % 2], s % 2, 2 * TILE)
+        project_values(hn.at[s % 2], s % 2, 2 * TILE)
+
+    def halo_attend(s):
         b, j = s // tiles, s % tiles
-        attend(b, slot, [bias[pl.ds(j, 1), :], bias[pl.ds(j + RIM_T + tiles, 1), :]], False)
-
-    with jax.named_scope("own0"):
-        own_project(0)
-    with jax.named_scope("own1"):
-        own_attend(0)
-        own_project(1)
-    pass_x(6)
-    pass_y(4)
-    with jax.named_scope("wait1"):
-        halo_wait(1)
-    with jax.named_scope("own2"):
-        own_attend(1)
-        halo_project(0)
-        halo_norm(1, 1)
-
-    def two_steps(t, _):
-        s = 2 * t
-        with jax.named_scope("wait2"):
-            halo_wait(s + 2)
-
-            @pl.when(t == 0)
-            def _():
-                pass_y(5)
-                pass_x(7)
-
-            @pl.when(t == 1)
-            def _():
-                pass_y(6)
-
-            @pl.when(t == 2)
-            def _():
-                pass_y(7)
-
-        with jax.named_scope("stepa"):
-            halo_attend(s, 0)
-            halo_project(1)
-            halo_norm(s + 2, 0)
-        with jax.named_scope("wait3"):
-            halo_wait(s + 3)
-
-            @pl.when(t == 0)
-            def _():
-                pass_x(8)
-
-            @pl.when(t == 2)
-            def _():
-                pass_y(8)
-
-        with jax.named_scope("stepb"):
-            halo_attend(s + 1, 1)
-            halo_project(0)
-            halo_norm(s + 3, 1)
-        return 0
-
-    lax.fori_loop(0, steps // 2 - 1, two_steps, 0)
-    with jax.named_scope("last"):
-        halo_attend(steps - 2, 0)
-        halo_project(1)
-        halo_attend(steps - 1, 1)
-    with jax.named_scope("gather2"):
-        arrive(1)
-        arrive(2)
-        arrive(3)
+        attend(b, s % 2, [bias[j:j + 1, :], bias[j + RIM_T + tiles:j + RIM_T + tiles + 1, :]], False)
 
     block = rows // 2
     inner = wu.shape[1]
     step = inner // 4
     slope = math.sqrt(2.0 / math.pi)
 
+    def merge(b):
+        for h in range(HEADS):
+            inverse = 1.0 / acc[b, h, head:head + 1, :]
+            blend[h * head:(h + 1) * head, :] = (acc[b, h, :head, :] * inverse).astype(BF16)
+
     def residual(b, r):
         at = slice(r * block, (r + 1) * block)
-        return (own[b, at, :].astype(F32) + dot_tn(blend[b, :, at], wo[...])).astype(BF16)
-
-    def feed(b, r, middle):
-        at = slice(r * block, (r + 1) * block)
-        second = normed(middle, gain2[...])
+        middle = (own[b, at, :].astype(F32) + dot_tn(blend[:, at], wo[...])).astype(BF16)
+        mid[r] = middle
+        second[r] = normed(middle, gain2[...])
+
+    def rise(r):
         for f in range(4):
-            u = dot_nn(second, wu[:, f * step:(f + 1) * step])
+            u = dot_nn(second[r], wu[:, f * step:(f + 1) * step])
             bent = jnp.tanh(u * (slope + (slope * 0.044715) * (u * u)))
             hid[r, :, f * step:(f + 1) * step] = (u + u * bent).astype(BF16)
-        out_ref[b, at, :] = (middle.astype(F32) + 0.5 * dot_nn(hid[r], wd[...])).astype(BF16)
-
+
+    def fall(b, r):
+        at = slice(r * block, (r + 1) * block)
+        out_ref[b, at, :] = (mid[r].astype(F32) + 0.5 * dot_nn(hid[r], wd[...])).astype(BF16)
+
+    index = {}
+    for p, entry in enumerate(pieces):
+        index[(entry[0], entry[2])] = p
+
+    def px(w, k):
+        with jax.named_scope(f"px{w}{k}"):
+            pass_x(index[(w, k)])
+
+    def py(w, k):
+        with jax.named_scope(f"py{w}{k}"):
+            pass_y(index[(w, k)])
+
+    def have(w):
+        with jax.named_scope(f"have{w}"):
+            arrive(w)
+
+    def halo_ready(s):
+        with jax.named_scope(f"halo{s}"):
+            halo_wait(s)
+
+    px(KEYS, 0)
+    px(KEYS, 1)
+    px(VALUES, 0)
+    px(VALUES, 1)
+    py(KEYS, 0)
+    px(QUERIES, 0)
+    py(KEYS, 1)
+    px(QUERIES, 1)
+    py(VALUES, 0)
+    have(KEYS)
+    with jax.named_scope("keys"):
+        for b in range(members):
+            project_keys(xn.at[b], 1 + b, rows)
+    py(VALUES, 1)
+    px(OUTPUT, 0)
+    py(QUERIES, 0)
+    have(VALUES)
+    with jax.named_scope("values"):
+        wv_t[...] = jnp.transpose(wv[...])
+        for b in range(members):
+            project_values(xn.at[b], 1 + b, rows)
+    py(QUERIES, 1)
+    halo_ready(0)
+    have(QUERIES)
+    with jax.named_scope("queries"):
+        wq_t[...] = jnp.transpose(wq[...])
+        project_queries(0)
+        halo_norm(0, 0)
+    px(UP, 0)
+    halo_ready(1)
+    with jax.named_scope("own0"):
+        own_attend(0)
+        project_queries(1)
+        halo_project(0)
+    py(OUTPUT, 0)
+    px(UP, 1)
+    with jax.named_scope("own1"):
+        own_attend(1)
+        halo_norm(1, 1)
+    halo_ready(2)
+    px(DOWN, 0)
+    with jax.named_scope("s0"):
+        halo_attend(0)
+        halo_project(1)
+        halo_norm(2, 0)
+    halo_ready(3)
+    py(UP, 0)
+    px(DOWN, 1)
+    with jax.named_scope("s1"):
+        halo_attend(1)
+        halo_project(2)
+        halo_norm(3, 1)
+    halo_ready(4)
+    with jax.named_scope("s2"):
+        halo_attend(2)
+        halo_project(3)
+        halo_norm(4, 0)
+    px(DOWN, 2)
+    py(UP, 1)
+    with jax.named_scope("s3"):
+        halo_attend(3)
+        merge(0)
+        halo_project(4)
+    px(DOWN, 3)
+    py(DOWN, 0)
+    have(OUTPUT)
+    halo_ready(5)
+    with jax.named_scope("s4"):
+        residual(0, 0)
+        residual(0, 1)
+        halo_attend(4)
+        halo_norm(5, 1)
+    py(DOWN, 1)
+    have(UP)
+    halo_ready(6)
+    with jax.named_scope("s5"):
+        rise(0)
+        halo_project(5)
+        halo_attend(5)
+        halo_norm(6, 0)
+    py(DOWN, 2)
+    with jax.named_scope("s6"):
+        rise(1)
+        halo_project(6)
+        halo_attend(6)
+    py(DOWN, 3)
+    halo_ready(7)
+    with jax.named_scope("s7a"):
+        halo_norm(7, 1)
+        halo_project(7)
+    have(DOWN)
+    with jax.named_scope("s7b"):
+        halo_attend(7)
+        fall(0, 0)
+        fall(0, 1)
+        merge(1)
     with jax.named_scope("finish"):
-        for b in range(members):
-            for h in range(HEADS):
-                inverse = 1.0 / acc[b, h, head:head + 1, :]
-                blend[b, h * head:(h + 1) * head, :] = (acc[b, h, :head, :] * inverse).astype(BF16)
-        jobs = [(b, r) for b in range(members) for r in range(2)]
-        middle = residual(*jobs[0])
-        for k, job in enumerate(jobs):
-            later = residual(*jobs[k + 1]) if k + 1 < len(jobs) else None
-            feed(*job, middle)
-            middle = later
+        residual(1, 0)
+        rise(0)
+        residual(1, 1)
+        fall(1, 0)
+        rise(1)
+        fall(1, 1)
 
     for b in range(members):
         for j in range(tiles):
             for side in range(2):
                 halo_copy(side, b, j).wait_send()
-    for w in range(4):
+    for w in range(n_weights):
         mate_copy(w, m).wait_send()
     for p in range(len(pieces)):
         x_copy(p, m).wait_send()
@@ -399,7 +447,9 @@
             scratch_shapes=[
                 pltpu.VMEM((members, rows, width), BF16),
                 pltpu.VMEM((members, 2, rows, width), BF16),
-                pltpu.VMEM((width, 3 * width), BF16),
+                pltpu.VMEM((width, width), BF16),
+                pltpu.VMEM((width, width), BF16),
+                pltpu.VMEM((width, width), BF16),
                 pltpu.VMEM((width, width), BF16),
                 pltpu.VMEM((width, inner), BF16),
                 pltpu.VMEM((inner, width), BF16),
@@ -408,19 +458,21 @@
                 pltpu.VMEM((members, rows, width), BF16),
                 pltpu.VMEM((2, 2 * TILE, width), BF16),
                 pltpu.VMEM((members, width, rows), BF16),
-                pltpu.VMEM((2, HEADS, rows, width // HEADS), BF16),
-                pltpu.VMEM((2, HEADS, width // HEADS + ONES, rows), BF16),
+                pltpu.VMEM((3, HEADS, rows, width // HEADS), BF16),
+                pltpu.VMEM((3, HEADS, width // HEADS + ONES, rows), BF16),
                 pltpu.VMEM((members, HEADS, width // HEADS + ONES, rows), F32),
                 pltpu.VMEM((members, HEADS, 1, rows), F32),
                 pltpu.VMEM((tiles + 2 * RIM_T, rows), F32),
                 pltpu.VMEM((HEADS, rows, rows), F32),
                 pltpu.VMEM((2, rows // 2, inner), BF16),
-                pltpu.VMEM((members, width, rows), BF16),
+                pltpu.VMEM((width, rows), BF16),
+                pltpu.VMEM((2, rows // 2, width), BF16),
+                pltpu.VMEM((2, rows // 2, width), BF16),
                 pltpu.VMEM((1, width), F32), pltpu.VMEM((1, width), F32),
                 pltpu.SMEM(lists.shape, jnp.int32), pltpu.SMEM(counts.shape, jnp.int32),
-                dma((9,)),
+                dma((11,)),
                 dma((2, members, tiles)), dma((2, members, tiles)),
-                dma((4,)), dma((4,)),
+                dma((6,)), dma((6,)),
             ] + [dma((n_pieces,)) for _ in range(8)],
             compiler_params=pltpu.CompilerParams(
                 collective_id=0, has_side_effects=True, vmem_limit_bytes=60 * 1024 * 1024

time: 44.1 us -> 44 us (level)
  no operation moved by 1% of the time
where the time goes in v4:
time: 44 us; the launch traced here: 43.9 us
  Pallas kernels  42.9 us (98%)
  local copies, waits for them, and re-layouts  0.97 us (2%)
    pallas_call x1, Pallas kernels, on_device(): pl.pallas_call(functools.partial(layer_kernel, geometry), name='layer', o...  42.9 us
    unnamed x1, local copies, waits for them, and re-layouts  0.97 us

profile of v4, /device:TPU:1, one launch (start us, length us, event | category | flops | bytes accessed | tf_op | source)
XLA Modules:
  0.0 43.9 jit_solution(12626957310046827189)
XLA Ops:
  0.0 42.9 %layer.1 = bf16[2,512,512]{2,1,0:T(8,128)(2,1)S(1)} custom-call(bf16[2,512,512]{2,1,0:T(8,128)(2,1)} %x_hbm.1, bf16[128,1536]{1,0:T(8,128)(2,1)} %wp_hbm.1, bf16[128,512]{1,0:T(8,128)(2,1)} %wo_hbm.1, bf16[128,2048]{1,0:T(8,128)(2,1)} %wu_hbm.1, bf16[512,512]{1,0:T(8,128)(2,1)} %wd_hbm.1, f32[1,512]{1,0:T(1,128)} %bitcast.2, f32[1,512]{1,0:T(1,128)} %bitcast.3, ...), custom_call_target="tpu_custom_call" | custom-call | tf_op jit(solution)/shard_map/layer/pallas_call | solution.py:441
  42.9 1.0 %copy.11 = bf16[2,512,512]{2,1,0:T(8,128)(2,1)} copy(bf16[2,512,512]{2,1,0:T(8,128)(2,1)S(1)} %layer.1) | data formatting | bytes 2097152

commit v5 on v4

v5 whole, which is shorter than its diff:
```python
import functools
import math

import jax
import jax.numpy as jnp
from jax import lax
from jax.experimental import pallas as pl
from jax.experimental.pallas import tpu as pltpu
from jax.sharding import PartitionSpec as P

HEADS = 4
TILE = 128
RIM_T = 4
HIDDEN_LOW = -1e30
ONES = 16
AHEAD = 4
MESH = pl.DeviceIdType.MESH
F32 = jnp.float32
BF16 = jnp.bfloat16

SPLIT = ((0, 2), (1, 2), (2, 2), (3, 1), (4, 2), (5, 4))
KEYS, VALUES, QUERIES, OUTPUT, UP, DOWN = range(6)


def normed(values, gain):
    values = values.astype(F32)
    center = values - jnp.mean(values, axis=-1, keepdims=True)
    spread = jnp.mean(center * center, axis=-1, keepdims=True)
    return (center * lax.rsqrt(spread + 1e-05) * gain).astype(BF16)


def dot_nn(a, b):
    return jnp.dot(a, b, preferred_element_type=F32)


def dot_nt(a, b):
    return lax.dot_general(a, b, (((1,), (1,)), ((), ())), preferred_element_type=F32)


def dot_tn(a, b):
    return lax.dot_general(a, b, (((0,), (0,)), ((), ())), preferred_element_type=F32)


def layer_kernel(
    geometry,
    x_hbm, wp_hbm, wo_hbm, wu_hbm, wd_hbm, gain1_hbm, gain2_hbm, lists_hbm, counts_hbm,
    out_ref,
    own, halo, wk, wv, wq, wo, wu, wd, wq_t, wv_t, xn, hn, q_t, kc, v_t, acc, top, bias, scores, hid, blend,
    second, mid,
    gain1, gain2, lists, counts,
    loc_sem, halo_send, halo_recv, weight_send, mate_recv, x_recv, y_recv,
):
    n_mesh, n_z, n_x, n_member = geometry
    members, rows, width = x_hbm.shape
    tiles = rows // TILE
    head = width // HEADS
    i = lax.axis_index("mesh")
    m = lax.axis_index("member")
    nxt = (i + 1) % n_mesh
    prv = (i + n_mesh - 1) % n_mesh
    x_lo = (i // n_z) % n_x
    y = i // (n_z * n_x)
    half = y % 2
    plane = n_z * n_x
    cross = (i + n_z - 2 * n_z * x_lo, (m + 2) % n_member)
    mate = (i, m + 1 - 2 * (m % 2))
    y_to = ((i + n_mesh + plane * (2 * x_lo - 1)) % n_mesh, m)
    y_from = ((i + n_mesh - plane * (2 * x_lo - 1)) % n_mesh, m)
    far = (m + 2) % n_member
    mate_far = (mate[1] + 2) % n_member

    barrier = pltpu.get_barrier_semaphore()
    for peer in ((nxt, m), (prv, m), cross, mate, y_to, y_from):
        pl.semaphore_signal(barrier, inc=1, device_id=peer, device_id_type=MESH)

    sources = (
        wp_hbm.at[:, pl.ds(width, width)], wp_hbm.at[:, pl.ds(2 * width, width)], wp_hbm.at[:, pl.ds(0, width)],
        wo_hbm, wu_hbm, wd_hbm,
    )
    fulls = (wk, wv, wq, wo, wu, wd)
    n_weights = len(fulls)

    def shard(w, owner):
        r = sources[w].shape[0]
        return fulls[w].at[pl.ds(pl.multiple_of(owner * r, 16), r), :]

    def piece(w, n, k, owner, which):
        r = sources[w].shape[0]
        size = r // 2 // n
        start = owner * r + which * (r // 2) + k * size
        return fulls[w].at[pl.ds(pl.multiple_of(start, 16), size), :]

    loads = [pltpu.make_async_copy(sources[w], shard(w, m), loc_sem.at[w]) for w in range(n_weights)]
    spots = [(0, slice(0, TILE)), (0, slice(TILE, rows)), (1, slice(0, rows))]
    load_x = [
        pltpu.make_async_copy(x_hbm.at[b, at, :], own.at[b, at, :], loc_sem.at[n_weights + 5 + k])
        for k, (b, at) in enumerate(spots)
    ]
    smalls = [
        pltpu.make_async_copy(src, dst, loc_sem.at[n_weights + 1 + k])
        for k, (src, dst) in enumerate(
            ((lists_hbm, lists), (counts_hbm, counts), (gain1_hbm, gain1), (gain2_hbm, gain2))
        )
    ]
    for load in load_x[:1] + loads[:3] + load_x[1:] + loads[3:] + smalls:
        load.start()

    pieces = []
    for w, n in SPLIT:
        for k in range(n):
            pieces.append((w, n, k))

    def remote(src, dst, send, recv, peer):
        return pltpu.make_async_remote_copy(
            src_ref=src, dst_ref=dst, send_sem=send, recv_sem=recv, device_id=peer, device_id_type=MESH
        )

    def halo_copy(side, b, j):
        raw = b == 0 and j == 0
        src = (own if raw else xn).at[b, pl.ds(j * TILE, TILE), :]
        dst = halo.at[b, j, pl.ds(side * TILE, TILE), :]
        peer = (nxt, m) if side == 0 else (prv, m)
        return remote(src, dst, halo_send.at[0], halo_recv.at[tiles * b + j], peer)

    def mate_copy(w, owner):
        return remote(shard(w, owner), shard(w, owner), weight_send.at[w], mate_recv.at[w], mate)

    def x_copy(p, owner):
        ref = piece(*pieces[p], owner, half)
        return remote(ref, ref, weight_send.at[pieces[p][0]], x_recv.at[p], cross)

    def y_copy(p, which):
        ref = piece(*pieces[p], far, which)
        return remote(ref, ref, weight_send.at[pieces[p][0]], y_recv.at[p], y_to)

    def d_copy(p, which):
        ref = piece(*pieces[p], far, which)
        return remote(ref, ref, weight_send.at[pieces[p][0]], mate_recv.at[pieces[p][0]], mate)

    def pass_x(p):
        x_copy(p, far).wait_recv()
        y_copy(p, half).start()
        d_copy(p, half).start()

    def pass_y(p):
        y_copy(p, 1 - half).wait_recv()
        d_copy(p, 1 - half).start()

    def arrive(w):
        both = fulls[w].at[pl.ds(0, 2 * sources[w].shape[0]), :]
        remote(both, both, weight_send.at[w], mate_recv.at[w], mate).wait_recv()

    def send_weight(w):
        loads[w].wait()
        for p, entry in enumerate(pieces):
            if entry[0] == w:
                x_copy(p, m).start()
        mate_copy(w, m).start()

    with jax.named_scope("enter"):
        pl.semaphore_wait(barrier, 6)
    load_x[0].wait()
    for side in range(2):
        halo_copy(side, 0, 0).start()
    send_weight(KEYS)
    send_weight(VALUES)
    send_weight(QUERIES)
    load_x[1].wait()
    load_x[2].wait()
    def norm_own(k, _):
        b = k // tiles
        at = pl.ds(pl.multiple_of((k % tiles) * TILE, TILE), TILE)
        xn[b, at, :] = normed(own[b, at, :], gain1[...])
        return 0

    with jax.named_scope("norm_own"):
        smalls[2].wait()
        smalls[3].wait()
        for b in range(members):
            lax.fori_loop(b * tiles, (b + 1) * tiles, norm_own, 0)
            for j in range(tiles):
                if b + j > 0:
                    for side in range(2):
                        halo_copy(side, b, j).start()
        send_weight(OUTPUT)
        send_weight(UP)
        send_weight(DOWN)
    for small in smalls[:2]:
        small.wait()
    first = i * tiles - RIM_T
    all_tiles = n_mesh * tiles
    entries = lists.shape[1]
    locals_ = [[(lists[t, e] - first + all_tiles) % all_tiles for e in range(entries)] for t in range(tiles)]
    for kt in range(tiles + 2 * RIM_T):
        for t in range(tiles):
            hit = jnp.int32(0)
            for e in range(entries):
                used = jnp.logical_and(locals_[t][e] == kt, e < counts[t])
                hit = jnp.where(used, jnp.int32(1), hit)
            level = jnp.where(hit > 0, F32(0), F32(HIDDEN_LOW))
            bias[pl.ds(kt, 1), t * TILE:(t + 1) * TILE] = jnp.full((1, TILE), level, F32)


    steps = members * tiles

    def norm_first(k):
        part = slice(k * (TILE // 2), (k + 1) * (TILE // 2))
        hn[part, :] = normed(halo[0, 0, part, :], gain1[...])

    first_jobs = [functools.partial(norm_first, k) for k in range(4)]

    def halo_wait(s):
        chunk = halo.at[s // tiles, s % tiles]
        remote(chunk, chunk, halo_send.at[0], halo_recv.at[s], (nxt, m)).wait_recv()

    scale = F32(math.log2(math.e) / math.sqrt(head))

    for slot in range(3):
        for h in range(HEADS):
            v_t[slot, h, head:, :] = jnp.ones((ONES, rows), BF16)

    wide = 2 * TILE
    spans = [slice(c * wide, (c + 1) * wide) for c in range(width // wide)]

    def key_jobs(source, slot, n):
        def job(span):
            keys = dot_nn(source[...], wk[:, span]).astype(BF16)
            for k in range(wide // head):
                kc[slot, span.start // head + k, :n, :] = keys[:, k * head:(k + 1) * head]

        return [functools.partial(job, span) for span in spans]

    def value_jobs(source, slot, n):
        def job(span):
            values = dot_nt(wv_t[span, :], source[...]).astype(BF16)
            for k in range(wide // head):
                v_t[slot, span.start // head + k, :head, :n] = values[k * head:(k + 1) * head, :]

        return [functools.partial(job, span) for span in spans]

    def query_jobs(b):
        def job(span):
            q_t[b, span, :] = (dot_nt(wq_t[span, :], xn[b]) * scale).astype(BF16)

        return [functools.partial(job, span) for span in spans]

    def attend_jobs(b, slot, marks, opening):
        n = len(marks) * TILE
        blocks = [(h, cols) for h in range(HEADS) for cols in spans]

        def score(h, cols):
            feats = slice(h * head, (h + 1) * head)
            scores[h, :n, cols] = dot_nn(kc[slot, h, :n, :], q_t[b, feats, cols])

        def blend_in(h, cols):
            best = None if opening else top[b, h, :, cols]
            for k, mark in enumerate(marks):
                high = jnp.max(scores[h, k * TILE:(k + 1) * TILE, cols], axis=0, keepdims=True) + mark[:, cols]
                best = high if best is None else jnp.maximum(best, high)
            parts = [
                jnp.exp2(scores[h, k * TILE:(k + 1) * TILE, cols] - (best - mark[:, cols])).astype(BF16)
                for k, mark in enumerate(marks)
            ]
            product = dot_nn(v_t[slot, h, :, :n], jnp.concatenate(parts, axis=0))
            if opening:
                acc[b, h, :, cols] = product
            else:
                acc[b, h, :, cols] = acc[b, h, :, cols] * jnp.exp2(top[b, h, :, cols] - best) + product
            top[b, h, :, cols] = best

        def job(k):
            if k == 0:
                for block in blocks[:AHEAD]:
                    score(*block)
            if k + AHEAD < len(blocks):
                score(*blocks[k + AHEAD])
            blend_in(*blocks[k])

        return [functools.partial(job, k) for k in range(len(blocks))]

    def own_jobs(b):
        return attend_jobs(b, 1 + b, [bias[RIM_T + t:RIM_T + t + 1, :] for t in range(tiles)], True)

    def project_jobs(s):
        source, slot = hn if s == 0 else halo.at[s // tiles, s % tiles], s % 2
        return key_jobs(source, slot, 2 * TILE) + value_jobs(source, slot, 2 * TILE)

    def halo_jobs(s):
        b, j = s // tiles, s % tiles
        return attend_jobs(b, s % 2, [bias[j:j + 1, :], bias[j + RIM_T + tiles:j + RIM_T + tiles + 1, :]], False)

    block_rows = rows // 2
    inner = wu.shape[1]
    slope = math.sqrt(2.0 / math.pi)

    def merge(b):
        for h in range(HEADS):
            inverse = 1.0 / acc[b, h, head:head + 1, :]
            blend[h * head:(h + 1) * head, :] = (acc[b, h, :head, :] * inverse).astype(BF16)

    def residual_jobs(b, r):
        part = block_rows // 2

        def job(k):
            at = slice(r * block_rows + k * part, r * block_rows + (k + 1) * part)
            to = slice(k * part, (k + 1) * part)
            middle = (own[b, at, :].astype(F32) + dot_tn(blend[:, at], wo[...])).astype(BF16)
            mid[2 * b + r, to, :] = middle
            second[2 * b + r, to, :] = normed(middle, gain2[...])

        return [functools.partial(job, k) for k in range(2)]

    def rise_jobs(b, r):
        def job(f):
            span = slice(f * wide, (f + 1) * wide)
            u = dot_nn(second[2 * b + r], wu[:, span])
            bent = jnp.tanh(u * (slope + (slope * 0.044715) * (u * u)))
            hid[2 * b + r, :, span] = (u + u * bent).astype(BF16)

        return [functools.partial(job, f) for f in range(inner // wide)]

    def fall_jobs(b, r):
        at = slice(r * block_rows, (r + 1) * block_rows)

        def job(span):
            down = dot_nn(hid[2 * b + r], wd[:, span])
            out_ref[b, at, span] = (mid[2 * b + r, :, span].astype(F32) + 0.5 * down).astype(BF16)

        return [functools.partial(job, span) for span in spans]

    def run(*queues):
        order = []
        for rank, queue in enumerate(queues):
            order += [((k + 0.5) / len(queue), rank, k) for k in range(len(queue))]
        for _, rank, k in sorted(order):
            queues[rank][k]()

    index = {}
    for p, entry in enumerate(pieces):
        index[(entry[0], entry[2])] = p

    def px(w, k):
        with jax.named_scope(f"px{w}{k}"):
            pass_x(index[(w, k)])

    def py(w, k):
        with jax.named_scope(f"py{w}{k}"):
            pass_y(index[(w, k)])

    def have(w):
        with jax.named_scope(f"have{w}"):
            arrive(w)

    def halo_ready(s):
        with jax.named_scope(f"halo{s}"):
            halo_wait(s)

    px(KEYS, 0)
    px(KEYS, 1)
    px(VALUES, 0)
    px(VALUES, 1)
    py(KEYS, 0)
    px(QUERIES, 0)
    py(KEYS, 1)
    px(QUERIES, 1)
    py(VALUES, 0)
    have(KEYS)
    with jax.named_scope("keys"):
        for b in range(members):
            run(key_jobs(xn.at[b], 1 + b, rows))
    py(VALUES, 1)
    px(OUTPUT, 0)
    py(QUERIES, 0)
    have(VALUES)
    py(QUERIES, 1)
    with jax.named_scope("values"):
        wv_t[...] = jnp.transpose(wv[...])
        for b in range(members):
            run(value_jobs(xn.at[b], 1 + b, rows))
    halo_ready(0)
    have(QUERIES)
    with jax.named_scope("queries"):
        wq_t[...] = jnp.transpose(wq[...])
        run(query_jobs(0), first_jobs)
    px(UP, 0)
    with jax.named_scope("own0"):
        run(own_jobs(0), query_jobs(1) + project_jobs(0))
    py(OUTPUT, 0)
    halo_ready(1)
    with jax.named_scope("own1"):
        run(own_jobs(1))
    px(UP, 1)
    with jax.named_scope("s0"):
        run(halo_jobs(0), project_jobs(1))
    halo_ready(2)
    px(DOWN, 0)
    with jax.named_scope("s1"):
        run(halo_jobs(1), project_jobs(2))
    py(UP, 0)
    halo_ready(3)
    with jax.named_scope("s2"):
        run(halo_jobs(2), project_jobs(3))
    px(DOWN, 1)
    halo_ready(4)
    with jax.named_scope("s3"):
        run(halo_jobs(3), project_jobs(4))
        merge(0)
    px(DOWN, 2)
    have(OUTPUT)
    with jax.named_scope("s4"):
        run(halo_jobs(4), residual_jobs(0, 0) + residual_jobs(0, 1))
    px(DOWN, 3)
    py(UP, 1)
    halo_ready(5)
    with jax.named_scope("s5"):
        run(project_jobs(5))
        run(halo_jobs(5))
    py(DOWN, 0)
    have(UP)
    with jax.named_scope("r00"):
        run(rise_jobs(0, 0))
    py(DOWN, 1)
    halo_ready(6)
    with jax.named_scope("s6"):
        run(project_jobs(6))
        run(halo_jobs(6), rise_jobs(0, 1)[:4])
    py(DOWN, 2)
    with jax.named_scope("r01"):
        run(rise_jobs(0, 1)[4:])
    halo_ready(7)
    py(DOWN, 3)
    with jax.named_scope("s7"):
        run(project_jobs(7))
        run(halo_jobs(7))
        merge(1)
        run(residual_jobs(1, 0))
    have(DOWN)
    with jax.named_scope("fin1"):
        run(rise_jobs(1, 0), residual_jobs(1, 1), fall_jobs(0, 0))
    with jax.named_scope("fin2"):
        run(rise_jobs(1, 1), fall_jobs(0, 1) + fall_jobs(1, 0))
        run(fall_jobs(1, 1))

    with jax.named_scope("sent"):
        remote(halo, halo, halo_send.at[0], halo_recv.at[0], (nxt, m)).wait_send()
        for w in range(n_weights):
            three = fulls[w].at[pl.ds(0, 3 * sources[w].shape[0]), :]
            remote(three, three, weight_send.at[w], mate_recv.at[w], mate).wait_send()


def solution(mesh):
    n_mesh, n_member = mesh.shape["mesh"], mesh.shape["member"]
    geometry = (n_mesh, 4, 2, n_member)

    def on_device(states, projection, output_w, up_w, down_w, gain1, gain2, lists, counts):
        members, rows, width = states.shape
        inner = up_w.shape[1]
        tiles = rows // TILE
        n_pieces = sum(n for _, n in SPLIT)
        hbm = pl.BlockSpec(memory_space=pl.ANY)
        vmem = pl.BlockSpec(memory_space=pltpu.VMEM)
        dma = pltpu.SemaphoreType.DMA
        return pl.pallas_call(
            functools.partial(layer_kernel, geometry),
            name="layer",
            out_shape=pltpu.VMEM(states.shape, BF16),
            in_specs=[hbm] * 9,
            out_specs=vmem,
            scratch_shapes=[
                pltpu.VMEM((members, rows, width), BF16),
                pltpu.VMEM((members, tiles, 2 * TILE, width), BF16),
                pltpu.VMEM((width, width), BF16),
                pltpu.VMEM((width, width), BF16),
                pltpu.VMEM((width, width), BF16),
                pltpu.VMEM((width, width), BF16),
                pltpu.VMEM((width, inner), BF16),
                pltpu.VMEM((inner, width), BF16),
                pltpu.VMEM((width, width), BF16),
                pltpu.VMEM((width, width), BF16),
                pltpu.VMEM((members, rows, width), BF16),
                pltpu.VMEM((2 * TILE, width), BF16),
                pltpu.VMEM((members, width, rows), BF16),
                pltpu.VMEM((3, HEADS, rows, width // HEADS), BF16),
                pltpu.VMEM((3, HEADS, width // HEADS + ONES, rows), BF16),
                pltpu.VMEM((members, HEADS, width // HEADS + ONES, rows), F32),
                pltpu.VMEM((members, HEADS, 1, rows), F32),
                pltpu.VMEM((tiles + 2 * RIM_T, rows), F32),
                pltpu.VMEM((HEADS, rows, rows), F32),
                pltpu.VMEM((4, rows // 2, inner), BF16),
                pltpu.VMEM((width, rows), BF16),
                pltpu.VMEM((4, rows // 2, width), BF16),
                pltpu.VMEM((4, rows // 2, width), BF16),
                pltpu.VMEM((1, width), F32), pltpu.VMEM((1, width), F32),
                pltpu.SMEM(lists.shape, jnp.int32), pltpu.SMEM(counts.shape, jnp.int32),
                dma((14,)),
                dma((1,)), dma((members * tiles,)),
                dma((6,)), dma((6,)), dma((n_pieces,)), dma((n_pieces,)),
            ],
            compiler_params=pltpu.CompilerParams(
                collective_id=0, has_side_effects=True, vmem_limit_bytes=60 * 1024 * 1024
            ),
        )(
            states, projection, output_w, up_w, down_w,
            gain1.reshape(1, width), gain2.reshape(1, width), lists, counts,
        )

    in_specs = (
        P("member", "mesh", None),
        P("member", None),
        P("member", None),
        P("member", None),
        P("member", None),
        P(),
        P(),
        P("mesh", None),
        P("mesh"),
    )
    return jax.shard_map(
        on_device, mesh=mesh, in_specs=in_specs, out_specs=P("member", "mesh", None), check_vma=False
    )
```

time: 44 us -> 40.1 us (0.911)
  Pallas kernels: 42.9 us -> 39.1 us
    pallas_call x1, Pallas kernels: 42.9 us -> 39.1 us  [on_device(): pl.pallas_call(functools.partial(layer_kernel, geometry), name='layer', o...]
where the time goes in v5:
time: 40.1 us; the launch traced here: 40 us
  Pallas kernels  39.1 us (98%)
  local copies, waits for them, and re-layouts  0.97 us (2%)
    pallas_call x1, Pallas kernels, on_device(): pl.pallas_call(functools.partial(layer_kernel, geometry), name='layer', o...  39.1 us
    unnamed x1, local copies, waits for them, and re-layouts  0.97 us

profile of v5, /device:TPU:1, one launch (start us, length us, event | category | flops | bytes accessed | tf_op | source)
XLA Modules:
  0.0 40.0 jit_solution(8574209941446360850)
XLA Ops:
  0.0 39.1 %layer.1 = bf16[2,512,512]{2,1,0:T(8,128)(2,1)S(1)} custom-call(bf16[2,512,512]{2,1,0:T(8,128)(2,1)} %x_hbm.1, bf16[128,1536]{1,0:T(8,128)(2,1)} %wp_hbm.1, bf16[128,512]{1,0:T(8,128)(2,1)} %wo_hbm.1, bf16[128,2048]{1,0:T(8,128)(2,1)} %wu_hbm.1, bf16[512,512]{1,0:T(8,128)(2,1)} %wd_hbm.1, f32[1,512]{1,0:T(1,128)} %bitcast.2, f32[1,512]{1,0:T(1,128)} %bitcast.3, ...), custom_call_target="tpu_custom_call" | custom-call | tf_op jit(solution)/shard_map/layer/pallas_call | solution.py:463
  39.1 1.0 %copy.11 = bf16[2,512,512]{2,1,0:T(8,128)(2,1)} copy(bf16[2,512,512]{2,1,0:T(8,128)(2,1)S(1)} %layer.1) | data formatting | bytes 2097152

commit v6 on v5

--- a/solution.py
+++ b/solution.py
@@ -19,6 +19,7 @@
 BF16 = jnp.bfloat16
 
 SPLIT = ((0, 2), (1, 2), (2, 2), (3, 1), (4, 2), (5, 4))
+DIRECT = ((5, 3),)
 KEYS, VALUES, QUERIES, OUTPUT, UP, DOWN = range(6)
 
 
@@ -137,9 +138,13 @@
         ref = piece(*pieces[p], far, which)
         return remote(ref, ref, weight_send.at[pieces[p][0]], mate_recv.at[pieces[p][0]], mate)
 
+    def straight(p):
+        return (pieces[p][0], pieces[p][2]) in DIRECT
+
     def pass_x(p):
         x_copy(p, far).wait_recv()
-        y_copy(p, half).start()
+        if not straight(p):
+            y_copy(p, half).start()
         d_copy(p, half).start()
 
     def pass_y(p):
@@ -155,6 +160,9 @@
         for p, entry in enumerate(pieces):
             if entry[0] == w:
                 x_copy(p, m).start()
+                if straight(p):
+                    ref = piece(*entry, m, 1 - half)
+                    remote(ref, ref, weight_send.at[w], y_recv.at[p], cross).start()
         mate_copy(w, m).start()
 
     with jax.named_scope("enter"):
@@ -371,8 +379,8 @@
     py(VALUES, 1)
     px(OUTPUT, 0)
     py(QUERIES, 0)
+    py(QUERIES, 1)
     have(VALUES)
-    py(QUERIES, 1)
     with jax.named_scope("values"):
         wv_t[...] = jnp.transpose(wv[...])
         for b in range(members):
@@ -424,13 +432,14 @@
     with jax.named_scope("s6"):
         run(project_jobs(6))
         run(halo_jobs(6), rise_jobs(0, 1)[:4])
+    py(DOWN, 3)
     py(DOWN, 2)
     with jax.named_scope("r01"):
         run(rise_jobs(0, 1)[4:])
     halo_ready(7)
-    py(DOWN, 3)
-    with jax.named_scope("s7"):
+    with jax.named_scope("s7a"):
         run(project_jobs(7))
+    with jax.named_scope("s7b"):
         run(halo_jobs(7))
         merge(1)
         run(residual_jobs(1, 0))

time: 40.1 us -> 39.4 us (0.983)
  Pallas kernels: 39.1 us -> 38.3 us
    pallas_call x1, Pallas kernels: 39.1 us -> 38.3 us  [on_device(): pl.pallas_call(functools.partial(layer_kernel, geometry), name='layer', o...]
where the time goes in v6:
time: 39.4 us; the launch traced here: 39.3 us
  Pallas kernels  38.3 us (97%)
  local copies, waits for them, and re-layouts  0.97 us (2%)
    pallas_call x1, Pallas kernels, on_device(): pl.pallas_call(functools.partial(layer_kernel, geometry), name='layer', o...  38.3 us
    unnamed x1, local copies, waits for them, and re-layouts  0.97 us

profile of v6, /device:TPU:1, one launch (start us, length us, event | category | flops | bytes accessed | tf_op | source)
XLA Modules:
  0.0 39.3 jit_solution(12812245814266329238)
XLA Ops:
  0.0 38.3 %layer.1 = bf16[2,512,512]{2,1,0:T(8,128)(2,1)S(1)} custom-call(bf16[2,512,512]{2,1,0:T(8,128)(2,1)} %x_hbm.1, bf16[128,1536]{1,0:T(8,128)(2,1)} %wp_hbm.1, bf16[128,512]{1,0:T(8,128)(2,1)} %wo_hbm.1, bf16[128,2048]{1,0:T(8,128)(2,1)} %wu_hbm.1, bf16[512,512]{1,0:T(8,128)(2,1)} %wd_hbm.1, f32[1,512]{1,0:T(1,128)} %bitcast.2, f32[1,512]{1,0:T(1,128)} %bitcast.3, ...), custom_call_target="tpu_custom_call" | custom-call | tf_op jit(solution)/shard_map/layer/pallas_call | solution.py:472
  38.3 1.0 %copy.11 = bf16[2,512,512]{2,1,0:T(8,128)(2,1)} copy(bf16[2,512,512]{2,1,0:T(8,128)(2,1)S(1)} %layer.1) | data formatting | bytes 2097152

commit v7 on v6

--- a/solution.py
+++ b/solution.py
@@ -13,7 +13,7 @@
 RIM_T = 4
 HIDDEN_LOW = -1e30
 ONES = 16
-AHEAD = 4
+AHEAD = 6
 MESH = pl.DeviceIdType.MESH
 F32 = jnp.float32
 BF16 = jnp.bfloat16
@@ -445,9 +445,9 @@
         run(residual_jobs(1, 0))
     have(DOWN)
     with jax.named_scope("fin1"):
-        run(rise_jobs(1, 0), residual_jobs(1, 1), fall_jobs(0, 0))
+        run(rise_jobs(1, 0), residual_jobs(1, 1), fall_jobs(0, 0) + fall_jobs(0, 1))
     with jax.named_scope("fin2"):
-        run(rise_jobs(1, 1), fall_jobs(0, 1) + fall_jobs(1, 0))
+        run(rise_jobs(1, 1), fall_jobs(1, 0))
         run(fall_jobs(1, 1))
 
     with jax.named_scope("sent"):

time: 39.4 us -> 39.4 us (level)
  no operation moved by 1% of the time
where the time goes in v7:
time: 39.4 us; the launch traced here: 39.3 us
  Pallas kernels  38.3 us (97%)
  local copies, waits for them, and re-layouts  0.97 us (2%)
    pallas_call x1, Pallas kernels, on_device(): pl.pallas_call(functools.partial(layer_kernel, geometry), name='layer', o...  38.3 us
    unnamed x1, local copies, waits for them, and re-layouts  0.97 us

profile of v7, /device:TPU:1, one launch (start us, length us, event | category | flops | bytes accessed | tf_op | source)
XLA Modules:
  0.0 39.3 jit_solution(14740776652539817695)
XLA Ops:
  0.0 38.3 %layer.1 = bf16[2,512,512]{2,1,0:T(8,128)(2,1)S(1)} custom-call(bf16[2,512,512]{2,1,0:T(8,128)(2,1)} %x_hbm.1, bf16[128,1536]{1,0:T(8,128)(2,1)} %wp_hbm.1, bf16[128,512]{1,0:T(8,128)(2,1)} %wo_hbm.1, bf16[128,2048]{1,0:T(8,128)(2,1)} %wu_hbm.1, bf16[512,512]{1,0:T(8,128)(2,1)} %wd_hbm.1, f32[1,512]{1,0:T(1,128)} %bitcast.2, f32[1,512]{1,0:T(1,128)} %bitcast.3, ...), custom_call_target="tpu_custom_call" | custom-call | tf_op jit(solution)/shard_map/layer/pallas_call | solution.py:472
  38.3 1.0 %copy.11 = bf16[2,512,512]{2,1,0:T(8,128)(2,1)} copy(bf16[2,512,512]{2,1,0:T(8,128)(2,1)S(1)} %layer.1) | data formatting | bytes 2097152
